TPU v7x, 32 devices: a whole 2x2x4 slice. The times are simulated.
32 devices in a mesh: dp: 8 (over z, y), bucket: 4 (over x, core).
Axes of the slice: x: 2, y: 2, z: 4, core: 2. Of those that a mesh axis runs over, the one named last changes fastest.
Arguments:
- tokens: bfloat16 [32768, 768], P(('dp', 'bucket')), may hold values from -6 to 6
- segment: int32 [64, 512], P(('dp', 'bucket')), may hold values from 0 to 8, as said below
- pair_order: int32 [512], replicated, may hold values from 0 to 511, each once
- cotangent: bfloat16 [32768, 768], P(('dp', 'bucket')), may hold values from -6 to 6
- query_weight: bfloat16 [768, 768], replicated, may hold values from -0.21875 to 0.21875
- query_bias: float32 [768], replicated, may hold values from -3 to 3
- key_weight: bfloat16 [768, 768], replicated, may hold values from -0.21875 to 0.21875
- value_weight: bfloat16 [768, 768], replicated, may hold values from -0.21875 to 0.21875
- value_bias: float32 [768], replicated, may hold values from -3 to 3
- out_weight: bfloat16 [768, 768], replicated, may hold values from -0.875 to 0.875
- out_bias: float32 [768], replicated, may hold values from -3 to 3
- norm_gain: float32 [768], replicated, may hold values from 0.5 to 1.5
- norm_shift: float32 [768], replicated, may hold values from -2 to 2
- inner_weight: bfloat16 [768, 3072], replicated, may hold values from -0.21875 to 0.21875
- inner_bias: float32 [3072], replicated, may hold values from -3 to 3
- outer_weight: bfloat16 [3072, 768], replicated, may hold values from -0.109375 to 0.109375
- outer_bias: float32 [768], replicated, may hold values from -3 to 3
- final_gain: float32 [768], replicated, may hold values from 0.5 to 1.5
- final_shift: float32 [768], replicated, may hold values from -0.6 to 0.6
Outputs:
- layer_out: bfloat16 [32768, 768], P(('dp', 'bucket'))
- loss_value: float32 [], replicated
- tokens_grad: float32 [32768, 768], P(('dp', 'bucket'))
- dquery_weight: float32 [768, 768], replicated
- dquery_bias: float32 [768], replicated
- dkey_weight: float32 [768, 768], replicated
- dvalue_weight: float32 [768, 768], replicated
- dvalue_bias: float32 [768], replicated
- dout_weight: float32 [768, 768], replicated
- dout_bias: float32 [768], replicated
- dnorm_gain: float32 [768], replicated
- dnorm_shift: float32 [768], replicated
- dinner_weight: float32 [768, 3072], replicated
- dinner_bias: float32 [3072], replicated
- douter_weight: float32 [3072, 768], replicated
- douter_bias: float32 [768], replicated
- dfinal_gain: float32 [768], replicated
- dfinal_shift: float32 [768], replicated
Inputs may be any that keep to these rules, and one draw needn't show every extreme that they name: In each packed row the segment numbers never fall; sentences 0 to 7 each hold one or more consecutive positions, then padding holds 8. Rows on devices whose bucket index is in the upper half hold sentences of up to 64 positions, the others of up to 32, and sentence 0 of every row has exactly that most. `pair_order`: A permutation of the sentences.
All inputs are finite; a program needn't handle non-finite values.
Results may differ from a plain program's by a relative error of at most 0.012.
Values sent between devices are 32-bit elements; how exact they have to be, the bound alone decides.
A program may use at most 256 MiB of HBM per device.

v0:
```python
import jax
import jax.numpy as jnp
from jax import lax
from jax.sharding import PartitionSpec as P

H = 12
HD = 64
S_ROW = 8


norm_eps = 1e-05
cos_scale = 20.0
masked_score = -1000000000.0


def layer_norm(hidden, gain, shift):
    centred = hidden - jnp.mean(hidden, axis=-1, keepdims=True)
    spread = lax.rsqrt(jnp.mean(centred * centred, axis=-1, keepdims=True) + norm_eps)
    return centred * spread * gain + shift


def gelu_exact(values):
    return jax.nn.gelu(values, approximate=False)


def matmul(left, right):
    return jnp.dot(left, right, preferred_element_type=jnp.float32)


def matmul_left(left, right):
    return lax.dot_general(
        left, right, (((0,), (0,)), ((), ())), preferred_element_type=jnp.float32
    )


def matmul_right(left, right):
    return lax.dot_general(
        left, right, (((1,), (1,)), ((), ())), preferred_element_type=jnp.float32
    )


def exact_dot(left, right, dims):
    return lax.dot_general(
        left,
        right,
        (dims, ((), ())),
        precision=lax.Precision.HIGHEST,
        preferred_element_type=jnp.float32,
    )


def to_sphere(vectors):
    factor = lax.rsqrt(jnp.sum(vectors * vectors, axis=1, keepdims=True) + 1e-06)
    return (vectors * factor, factor)


def sphere_back(unit, factor, upstream):
    return factor * (upstream - unit * jnp.sum(unit * upstream, axis=1, keepdims=True))


def masked_scores(query_h, key_h, same):
    raw = jnp.einsum("rqhe,rkhe->rhqk", query_h, key_h, preferred_element_type=jnp.float32) * 0.125
    return jnp.where(same, raw, jnp.float32(masked_score))


def row_logsum(logits):
    top = jnp.max(logits, axis=1, keepdims=True)
    return top + jnp.log(jnp.sum(jnp.exp(logits - top), axis=1, keepdims=True))


def local(
    tokens,
    segment,
    pair_order,
    cotangent,
    query_weight,
    query_bias,
    key_weight,
    value_weight,
    value_bias,
    out_weight,
    out_bias,
    norm_gain,
    norm_shift,
    inner_weight,
    inner_bias,
    outer_weight,
    outer_bias,
    final_gain,
    final_shift,
):
    nrows = segment.shape[0]
    seqlen = segment.shape[1]
    width = tokens.shape[1]
    query_b = (matmul(tokens, query_weight) + query_bias).astype(jnp.bfloat16)
    key_b = matmul(tokens, key_weight).astype(jnp.bfloat16)
    value_b = (matmul(tokens, value_weight) + value_bias).astype(jnp.bfloat16)
    query_h = query_b.reshape(nrows, seqlen, H, HD)
    key_h = key_b.reshape(nrows, seqlen, H, HD)
    value_h = value_b.reshape(nrows, seqlen, H, HD)
    same = segment[:, None, :, None] == segment[:, None, None, :]
    scores = masked_scores(query_h, key_h, same)
    peak = jnp.max(scores, axis=-1, keepdims=True)
    log_total = peak + jnp.log(jnp.sum(jnp.exp(scores - peak), axis=-1, keepdims=True))
    probs_b = jnp.exp(scores - log_total).astype(jnp.bfloat16)
    context = jnp.einsum("rhqk,rkhe->rqhe", probs_b, value_h, preferred_element_type=jnp.float32)
    context_b = context.astype(jnp.bfloat16).reshape(nrows * seqlen, width)
    first = tokens.astype(jnp.float32) + matmul(context_b, out_weight) + out_bias
    normed, norm_back = jax.vjp(layer_norm, first, norm_gain, norm_shift)
    normed_b = normed.astype(jnp.bfloat16)
    inner = matmul(normed_b, inner_weight) + inner_bias
    active, gelu_back = jax.vjp(gelu_exact, inner)
    active_b = active.astype(jnp.bfloat16)
    second = normed + matmul(active_b, outer_weight) + outer_bias
    final, final_back = jax.vjp(layer_norm, second, final_gain, final_shift)
    layer_out = final.astype(jnp.bfloat16)
    onehot = (segment[:, None, :] == jnp.arange(S_ROW, dtype=jnp.int32)[None, :, None]).astype(
        jnp.float32
    )
    counts = jnp.sum(onehot, axis=2, keepdims=True)
    pooled = (
        jnp.einsum(
            "rsl,rld->rsd",
            onehot,
            final.reshape(nrows, seqlen, width),
            precision=lax.Precision.HIGHEST,
        )
        / counts
    )
    pooled = pooled.reshape(nrows * S_ROW, width)
    pooled_every = lax.all_gather(pooled, ("dp", "bucket"), axis=0, tiled=True)
    sents = pooled_every.shape[0]
    pairs = sents // 2
    device = lax.axis_index(("dp", "bucket"))
    ordered = pooled_every[pair_order]
    unit_p, factor_p = to_sphere(ordered[pairs:])
    share = pairs // lax.axis_size(("dp", "bucket"))
    first_pair = device * share
    unit_a, factor_a = to_sphere(lax.dynamic_slice_in_dim(ordered, first_pair, share, 0))
    logits = cos_scale * exact_dot(unit_a, unit_p, ((1,), (1,)))
    log_sum = row_logsum(logits)
    diagonal = jnp.diagonal(lax.dynamic_slice_in_dim(logits, first_pair, share, 1))
    loss_value = lax.psum(jnp.sum(log_sum[:, 0] - diagonal), ("dp", "bucket"))
    columns = jnp.arange(pairs, dtype=jnp.int32)[None, :]
    targets = (first_pair + jnp.arange(share, dtype=jnp.int32))[:, None]
    weighting = jnp.exp(logits - log_sum) - (columns == targets).astype(jnp.float32)
    grad_anchor = sphere_back(
        unit_a, factor_a, cos_scale * exact_dot(weighting, unit_p, ((1,), (0,)))
    )
    grad_positive = sphere_back(
        unit_p, factor_p, cos_scale * exact_dot(weighting, unit_a, ((0,), (0,)))
    )
    dense = jnp.zeros((sents, width), jnp.float32).at[pair_order[pairs:]].set(grad_positive)
    dense = dense.at[lax.dynamic_slice_in_dim(pair_order, first_pair, share, 0)].set(grad_anchor)
    dpooled = lax.psum_scatter(dense, ("dp", "bucket"), scatter_dimension=0, tiled=True)
    spread_back = jnp.einsum(
        "rsl,rsd->rld",
        onehot,
        dpooled.reshape(nrows, S_ROW, width) / counts,
        precision=lax.Precision.HIGHEST,
    )
    grad_final = cotangent.astype(jnp.float32) + spread_back.reshape(nrows * seqlen, width)
    grad_second, dfinal_gain, dfinal_shift = final_back(grad_final)
    grad_second_b = grad_second.astype(jnp.bfloat16)
    douter_weight = matmul_left(active_b, grad_second_b)
    douter_bias = jnp.sum(grad_second, axis=0)
    (grad_inner,) = gelu_back(matmul_right(grad_second_b, outer_weight))
    grad_inner_b = grad_inner.astype(jnp.bfloat16)
    dinner_weight = matmul_left(normed_b, grad_inner_b)
    dinner_bias = jnp.sum(grad_inner, axis=0)
    grad_normed = grad_second + matmul_right(grad_inner_b, inner_weight)
    grad_first, dnorm_gain, dnorm_shift = norm_back(grad_normed)
    grad_first_b = grad_first.astype(jnp.bfloat16)
    dout_weight = matmul_left(context_b, grad_first_b)
    dout_bias = jnp.sum(grad_first, axis=0)
    grad_context = (
        matmul_right(grad_first_b, out_weight).astype(jnp.bfloat16).reshape(nrows, seqlen, H, HD)
    )
    scores = masked_scores(query_h, key_h, same)
    probs = jnp.exp(scores - log_total)
    probs_b = probs.astype(jnp.bfloat16)
    grad_probs = jnp.einsum(
        "rqhe,rkhe->rhqk", grad_context, value_h, preferred_element_type=jnp.float32
    )
    grad_value = jnp.einsum(
        "rhqk,rqhe->rkhe", probs_b, grad_context, preferred_element_type=jnp.float32
    )
    grad_scores = probs * (grad_probs - jnp.sum(probs * grad_probs, axis=-1, keepdims=True))
    grad_scores_b = grad_scores.astype(jnp.bfloat16)
    grad_query = (
        jnp.einsum("rhqk,rkhe->rqhe", grad_scores_b, key_h, preferred_element_type=jnp.float32)
        * 0.125
    )
    grad_key = (
        jnp.einsum("rhqk,rqhe->rkhe", grad_scores_b, query_h, preferred_element_type=jnp.float32)
        * 0.125
    )
    grad_query = grad_query.reshape(nrows * seqlen, width)
    grad_key = grad_key.reshape(nrows * seqlen, width)
    grad_value = grad_value.reshape(nrows * seqlen, width)
    dquery_bias = jnp.sum(grad_query, axis=0)
    dvalue_bias = jnp.sum(grad_value, axis=0)
    grad_query_b = grad_query.astype(jnp.bfloat16)
    grad_key_b = grad_key.astype(jnp.bfloat16)
    grad_value_b = grad_value.astype(jnp.bfloat16)
    dquery_weight = matmul_left(tokens, grad_query_b)
    dkey_weight = matmul_left(tokens, grad_key_b)
    dvalue_weight = matmul_left(tokens, grad_value_b)
    tokens_grad = (
        grad_first
        + matmul_right(grad_query_b, query_weight)
        + matmul_right(grad_key_b, key_weight)
        + matmul_right(grad_value_b, value_weight)
    )
    (
        dquery_weight,
        dquery_bias,
        dkey_weight,
        dvalue_weight,
        dvalue_bias,
        dout_weight,
        dout_bias,
        dnorm_gain,
        dnorm_shift,
        dinner_weight,
        dinner_bias,
        douter_weight,
        douter_bias,
        dfinal_gain,
        dfinal_shift,
    ) = lax.psum(
        (
            dquery_weight,
            dquery_bias,
            dkey_weight,
            dvalue_weight,
            dvalue_bias,
            dout_weight,
            dout_bias,
            dnorm_gain,
            dnorm_shift,
            dinner_weight,
            dinner_bias,
            douter_weight,
            douter_bias,
            dfinal_gain,
            dfinal_shift,
        ),
        ("dp", "bucket"),
    )
    return (
        layer_out,
        loss_value,
        tokens_grad,
        dquery_weight,
        dquery_bias,
        dkey_weight,
        dvalue_weight,
        dvalue_bias,
        dout_weight,
        dout_bias,
        dnorm_gain,
        dnorm_shift,
        dinner_weight,
        dinner_bias,
        douter_weight,
        douter_bias,
        dfinal_gain,
        dfinal_shift,
    )


def solution(mesh):
    return jax.shard_map(
        local,
        mesh=mesh,
        in_specs=(
            P(("dp", "bucket"), None),
            P(("dp", "bucket"), None),
            P(),
            P(("dp", "bucket"), None),
            P(),
            P(),
            P(),
            P(),
            P(),
            P(),
            P(),
            P(),
            P(),
            P(),
            P(),
            P(),
            P(),
            P(),
            P(),
        ),
        out_specs=(
            P(("dp", "bucket"), None),
            P(),
            P(("dp", "bucket"), None),
            P(),
            P(),
            P(),
            P(),
            P(),
            P(),
            P(),
            P(),
            P(),
            P(),
            P(),
            P(),
            P(),
            P(),
            P(),
        ),
        check_vma=False,
    )
```

profile of v0, /device:TPU:0, one launch (start us, length us, event | category | flops | bytes accessed | tf_op | source)
XLA Modules:
  0.0 910.1 jit_solution(1644720705829579922)
XLA Ops:
  9.2 4.3 add_convert_fusion.1
  15.2 2.4 reshape.187
  17.6 3.1 convolution_convert_fusion.2
  22.4 2.9 reshape.189
  25.3 4.8 add_convert_fusion
  30.1 2.6 copy.53
  32.7 3.8 reshape.188
  36.6 12.0 %fusion = (f32[2,12,512]{2,1,0:T(8,128)S(1)}, f32[2,12,512,512]{2,3,1,0:T(8,128)}) fusion(pred[2,512,512]{1,2,0:T(8,128)(4,1)S(1)} %broadcast_compare_fusion, bf16[2,512,12,64]{1,0,3,2:T(2,128)(2,1)S(1)} %reshape.189, bf16[2,512,12,64]{1,0,3,2:T(2,128)(2,1)} %reshape.188), kind=kOutput, calls=%fused_computation.9 | convolution fusion | flops 824168448 | bytes 28884992 | tf_op jit(solution)/shard_map/rqhe,rkhe->rhqk/dot_general | solution.py:62
  48.6 11.1 %exponential_reduce_fusion = f32[2,12,512]{2,1,0:T(8,128)S(1)} fusion(f32[2,12,512,512]{2,3,1,0:T(8,128)} %get-tuple-element.87, f32[2,12,512]{2,1,0:T(8,128)S(1)} %get-tuple-element.86, pred[2,512,512]{1,2,0:T(8,128)(4,1)S(1)} %broadcast_compare_fusion), kind=kLoop, calls=%fused_computation.7 | loop fusion | flops 25153536 | bytes 25788416 | tf_op jit(solution)/shard_map/reduce_sum | solution.py:104
  59.8 11.9 %fusion.15 = bf16[2,512,12,64]{1,3,2,0:T(8,128)(2,1)S(1)} fusion(bf16[2,512,12,64]{1,0,3,2:T(2,128)(2,1)S(1)} %copy-done.16, f32[2,12,512,512]{2,3,1,0:T(8,128)} %get-tuple-element.87, f32[2,12,512]{2,1,0:T(8,128)S(1)} %log_add_fusion, pred[2,512,512]{1,2,0:T(8,128)(4,1)S(1)} %broadcast_compare_fusion), kind=kOutput, calls=%fused_computation.65 | convolution fusion | flops 831258624 | bytes 28884992 | tf_op jit(solution)/shard_map/rhqk,rkhe->rqhe/dot_general | solution.py:106
  78.2 35.0 %multiply_convert_fusion.1 = (bf16[1024,3072]{1,0:T(8,128)(2,1)S(1)}, f32[1024,3072]{1,0:T(8,128)}, f32[1024,3072]{1,0:T(8,128)}) fusion(f32[3072]{0:T(1024)S(1)} %copy-done.57, bf16[768,3072]{1,0:T(8,128)(2,1)S(1)} %bitcast.116, f32[1024,768]{1,0:T(8,128)S(1)} %get-tuple-element.89, f32[768]{0:T(1024)S(1)} %copy-done.39, f32[768]{0:T(1024)S(1)} %copy-done.35, ...), kind=kOutput, calls=%fused_computation.14 | convolution fusion | flops 5043388416 | bytes 39348224 | tf_op jit(solution)/shard_map/dot_general | solution.py:27
  113.2 5.4 fusion.76
  124.8 55.9 %all-gather.2.cloned.1.call-done = f32[512,768]{1,0:T(8,128)} async-done(((f32[16,768]{1,0:T(8,128)}), f32[512,768]{1,0:T(8,128)}) %all-gather.2.cloned.1.call-update) | async-done | bytes 1572880 | tf_op jit(solution)/shard_map/all_gather | solution.py:131
  180.7 3.9 gather_fusion
  187.4 2.4 multiply_reduce_fusion.7
  189.8 2.5 multiply_reduce_fusion.9
  192.3 3.1 scatter_custom_fusion
  195.4 3.5 scatter_custom_fusion.1
  199.2 96.8 %reduce-scatter.2.cloned.1.call-done = f32[16,768]{1,0:T(8,128)} async-done(((f32[512,768]{1,0:T(8,128)}), f32[16,768]{1,0:T(8,128)}) %reduce-scatter.2.cloned.1.call-update) | async-done | bytes 49168 | tf_op jit(solution)/shard_map/reduce_scatter | solution.py:155
  296.0 2.4 fusion.40
  298.4 2.6 multiply_reduce_fusion.1
  301.0 2.9 fusion.72
  303.9 18.8 %fusion.78 = (f32[3072]{0:T(1024)S(1)}, bf16[1024,3072]{1,0:T(8,128)(2,1)}) fusion(f32[1024,3072]{1,0:T(8,128)} %get-tuple-element.85, bf16[3072,768]{1,0:T(8,128)(2,1)} %param.34, f32[1024,768]{1,0:T(8,128)} %get-tuple-element.79, f32[1024]{0:T(1024)S(1)} %negate_multiply_fusion.2, f32[1024,3072]{1,0:T(8,128)} %get-tuple-element.90, f32[3072]{0:T(1024)S(1)} %copy-done.58), kind=kOutput, calls=%fused_computation.160 | convolution fusion | flops 4883739648 | bytes 39350272 | tf_op jit(solution)/shard_map/dot_general | solution.py:37
  322.8 11.0 %multiply_reduce_fusion.2 = (f32[768]{0:T(1024)S(1)}, f32[1024]{0:T(1024)S(1)}, f32[768]{0:T(1024)S(1)}, f32[1024,768]{1,0:T(8,128)S(1)}) fusion(f32[1024,768]{1,0:T(8,128)} %copy-done.4, f32[1024]{0:T(1024)S(1)} %fusion.58, f32[1024]{0:T(1024)S(1)} %broadcast_multiply_fusion.1, f32[768]{0:T(1024)S(1)} %copy-done.36, bf16[768,3072]{1,0:T(8,128)(2,1)} %param.32, ...), kind=kOutput, calls=%fused_computation.36 | convolution fusion | flops 4839699456 | bytes 20472832 | tf_op jit(solution)/shard_map/dot_general | solution.py:37
  336.9 2.6 convolution_convert_fusion.1
  339.5 2.7 copy.60
  342.3 3.8 reshape.195
  346.1 18.4 %multiply_reduce_fusion = (f32[2,12,512]{2,1,0:T(8,128)S(1)}, f32[2,12,512,512]{2,3,1,0:T(8,128)}) fusion(f32[2,12,512,512]{2,3,1,0:T(8,128)} %get-tuple-element.87, f32[2,12,512]{2,1,0:T(8,128)S(1)} %copy-done.29, pred[2,512,512]{1,2,0:T(8,128)(4,1)S(1)} %copy-done.14, bf16[2,512,12,64]{1,0,3,2:T(2,128)(2,1)S(1)} %copy-done.17, ...), kind=kOutput, calls=%fused_computation.5 | convolution fusion | flops 836751360 | bytes 54099968 | tf_op jit(solution)/shard_map/rqhe,rkhe->rhqk/dot_general | solution.py:182
  364.6 12.6 %bitcast_reduce_fusion = (f32[12,64]{1,0:T(8,128)S(1)}, bf16[2,12,64,512]{3,2,1,0:T(8,128)(2,1)}) fusion(f32[2,12,512,512]{2,3,1,0:T(8,128)} %get-tuple-element.87, f32[2,12,512]{2,1,0:T(8,128)S(1)} %copy-done.29, pred[2,512,512]{1,2,0:T(8,128)(4,1)S(1)} %copy-done.14, bf16[2,512,12,64]{1,0,3,2:T(2,128)(2,1)} %reshape.195), kind=kOutput, calls=%fused_computation.30 | convolution fusion | flops 832044288 | bytes 28888064 | tf_op jit(solution)/shard_map/rhqk,rqhe->rkhe/dot_general | solution.py:185
  377.2 17.4 %multiply_convert_fusion = bf16[2,12,512,512]{2,3,1,0:T(8,128)(2,1)S(1)} fusion(f32[2,12,512,512]{2,3,1,0:T(8,128)} %get-tuple-element.101, f32[2,12,512,512]{2,3,1,0:T(8,128)} %get-tuple-element.87, f32[2,12,512]{2,1,0:T(8,128)S(1)} %get-tuple-element.100, f32[2,12,512]{2,1,0:T(8,128)S(1)} %copy-done.29, pred[2,512,512]{1,2,0:T(8,128)(4,1)S(1)} %copy-done.14), kind=kLoop, calls=%fused_computation.4 | loop fusion | flops 37748736 | bytes 63537152 | tf_op jit(solution)/shard_map/convert_element_type | solution.py:189
  394.6 4.5 copy-done.1
  399.1 2.2 bitcast_reduce_fusion.1
  401.3 9.8 %fusion.16 = bf16[2,512,12,64]{1,3,2,0:T(8,128)(2,1)} fusion(bf16[2,12,512,512]{2,3,1,0:T(8,128)(2,1)} %copy-done.1, bf16[2,512,12,64]{1,0,3,2:T(2,128)(2,1)S(1)} %copy-done.12), kind=kOutput, calls=%fused_computation.66 | convolution fusion | flops 806879232 | bytes 15728640 | tf_op jit(solution)/shard_map/rhqk,rqhe->rkhe/dot_general | solution.py:195
  411.1 4.5 fusion.67
  415.6 10.9 %fusion.8 = f32[768,3072]{1,0:T(8,128)} fusion(bf16[1024,3072]{1,0:T(8,128)(2,1)} %get-tuple-element.107, f32[1024,768]{1,0:T(8,128)S(1)} %copy-done.6, f32[768]{0:T(1024)S(1)} %copy-done.40, f32[768]{0:T(1024)S(1)} %copy-done.36, f32[1024]{0:T(1024)S(1)} %fusion.58, f32[1024]{0:T(1024)S(1)} %broadcast_multiply_fusion.1), kind=kOutput, calls=%fused_computation.40 | convolution fusion | flops 4835770368 | bytes 18888704 | tf_op jit(solution)/shard_map/dot_general | solution.py:31
  426.5 8.2 fusion.66
  441.5 2.8 convolution_bitcast_fusion.2
  444.3 2.8 convolution_bitcast_fusion.1
  447.0 2.8 convolution_bitcast_fusion
  450.0 3.4 add_reduce_fusion
  453.4 43.7 %all-reduce = (f32[]{:T(128)}, f32[768]{0:T(1024)}, f32[768]{0:T(1024)}, f32[768]{0:T(1024)}, f32[768]{0:T(1024)}, /*index=5*/f32[768]{0:T(1024)}, f32[3072]{0:T...) all-reduce(f32[]{:T(128)} %get-tuple-element.80, ...), channel_id=1, replica_groups=mesh['dp'=8,'bucket'=4] {'dp','bucket'}, use_global_device_ids=true, to_apply=%region_12.13 | all-reduce | flops 9217 | bytes 73736 | tf_op jit(solution)/shard_map/psum | solution.py:143
  497.1 3.4 fusion.80
  503.1 3.6 add_add_fusion.2
  506.7 373.7 %all-reduce.4.cloned.1.call-done = (f32[768,768]{0,1:T(8,128)}, f32[768,768]{0,1:T(8,128)}, f32[768,768]{0,1:T(8,128)}, f32[768,768]{1,0:T(8,128)}, f32[768,3072]{1,0:T(8,128)}, /*index=5*/f32[3072,768]{1,0:T(8,128)}) async-done(((f32[768,768]{0,1:T(8,128)}, f32[768,768]{0,1:T(8,128)}, f32[768,768]{0,1:T(8,128)}, f32[768,768]{1,0:T(8,128)}, f32[768,3072]{1,0:T(8,128)}, /*index=5*/f32[3072,768]{1,0:T(8,128)}), ...) | async-done | bytes 28311568 | tf_op jit(solution)/shard_map/psum | solution.py:231
  880.4 3.2 copy.72
  885.5 3.2 copy.74
  890.1 9.3 %copy.119 = f32[768,3072]{1,0:T(8,128)} copy(f32[768,3072]{1,0:T(8,128)} %get-tuple-element.126) | data formatting | bytes 18874368
  899.4 3.7 copy.120
  (201 shorter events, 36.7 us)
Async XLA Ops:
  7.2 66.6 %copy-start = (bf16[768,768]{1,0:T(8,128)(2,1)S(1)}, bf16[768,768]{1,0:T(8,128)(2,1)}, u32[]{:S(2)}) copy-start(bf16[768,768]{1,0:T(8,128)(2,1)} %param.28) | copy-start | bytes 3538948
  7.2 173.5 %all-gather.2.cloned.1.call-start = ((), (), s32[]{:S(2)}) async-start(), calls=%async_computation.1 | async-start | bytes 1622016 | tf_op jit(solution)/shard_map/all_gather | solution.py:131
  8.4 51.3 %copy-start.13 = (pred[2,512,512]{1,2,0:T(8,128)(4,1)}, pred[2,512,512]{1,2,0:T(8,128)(4,1)S(1)}, u32[]{:S(2)}) copy-start(pred[2,512,512]{1,2,0:T(8,128)(4,1)S(1)} %broadcast_compare_fusion) | copy-start | bytes 1572868
  9.2 112.0 %copy-start.48 = (f32[2,8]{1,0:T(2,128)}, f32[2,8]{1,0:T(2,128)S(1)}, u32[]{:S(2)}) copy-start(f32[2,8]{1,0:T(2,128)S(1)} %convert_reduce_fusion) | copy-start | bytes 196
  20.7 4.5 copy-start.59
  25.3 11.3 %copy-start.10 = (bf16[2,512,12,64]{1,0,3,2:T(2,128)(2,1)}, bf16[2,512,12,64]{1,0,3,2:T(2,128)(2,1)S(1)}, u32[]{:S(2)}) copy-start(bf16[2,512,12,64]{1,0,3,2:T(2,128)(2,1)S(1)} %reshape.189) | copy-start | bytes 4718596
  48.6 11.2 %copy-start.16 = (bf16[2,512,12,64]{1,0,3,2:T(2,128)(2,1)S(1)}, bf16[2,512,12,64]{1,0,3,2:T(2,128)(2,1)}, u32[]{:S(2)}) copy-start(bf16[2,512,12,64]{1,0,3,2:T(2,128)(2,1)} %reshape.187) | copy-start | bytes 4718596
  59.8 11.9 %copy-start.28 = (f32[2,12,512]{2,1,0:T(8,128)}, f32[2,12,512]{2,1,0:T(8,128)S(1)}, u32[]{:S(2)}) copy-start(f32[2,12,512]{2,1,0:T(8,128)S(1)} %log_add_fusion) | copy-start | bytes 147460
  73.8 3.4 slice-start.6
  73.8 39.4 %slice-start.3 = ((s8[4718592]{0:T(1024)(128)(4,1)}), s8[4194304]{0:T(1024)(128)(4,1)S(1)}, s32[]{:S(2)}) async-start(s8[4718592]{0:T(1024)(128)(4,1)} %bitcast.113), calls=%async_computation.7 | async-start | bytes 8388608
  75.5 37.7 %copy-start.4 = (f32[1024,768]{1,0:T(8,128)}, f32[1024,768]{1,0:T(8,128)S(1)}, u32[]{:S(2)}) copy-start(f32[1024,768]{1,0:T(8,128)S(1)} %get-tuple-element.89) | copy-start | bytes 9437188
  78.2 35.0 %slice-start.4 = ((s8[4718592]{0:T(1024)(128)(4,1)}), s8[524288]{0:T(1024)(128)(4,1)S(1)}, s32[]{:S(2)}) async-start(s8[4718592]{0:T(1024)(128)(4,1)} %bitcast.113), calls=%async_computation.8 | async-start | bytes 1048576
  78.2 35.0 %copy-start.61 = (f32[768]{0:T(1024)S(1)}, f32[768]{0:T(1024)}, u32[]{:S(2)}) copy-start(f32[768]{0:T(1024)} %param.35) | copy-start | bytes 9220
  113.2 5.5 copy-start.62
  123.0 172.9 %reduce-scatter.2.cloned.1.call-start = ((), (), s32[]{:S(2)}) async-start(), calls=%async_computation.2 | async-start | bytes 1622016 | tf_op jit(solution)/shard_map/reduce_scatter | solution.py:155
  187.4 8.0 copy-start.51
  195.4 100.6 %copy-start.32 = (s32[2,512]{1,0:T(2,128)S(1)}, s32[2,512]{1,0:T(2,128)}, u32[]{:S(2)}) copy-start(s32[2,512]{1,0:T(2,128)} %param.20) | copy-start | bytes 12292
  195.4 100.6 %copy-start.49 = (f32[2,8]{1,0:T(2,128)S(1)}, f32[2,8]{1,0:T(2,128)}, u32[]{:S(2)}) copy-start(f32[2,8]{1,0:T(2,128)} %copy-done.48) | copy-start | bytes 196
  195.4 103.0 %copy-start.34 = (f32[1024]{0:T(1024)S(1)}, f32[1024]{0:T(1024)}, u32[]{:S(2)}) copy-start(f32[1024]{0:T(1024)} %copy-done.33) | copy-start | bytes 12292
  195.4 103.0 %copy-start.38 = (f32[768]{0:T(1024)S(1)}, f32[768]{0:T(1024)}, u32[]{:S(2)}) copy-start(f32[768]{0:T(1024)} %param.36) | copy-start | bytes 9220
  198.9 99.5 %copy-start.18 = (bf16[1024,768]{1,0:T(8,128)(2,1)S(1)}, bf16[1024,768]{1,0:T(8,128)(2,1)}, u32[]{:S(2)}) copy-start(bf16[1024,768]{1,0:T(8,128)(2,1)} %param.22) | copy-start | bytes 4718596
  198.9 681.4 %all-reduce.4.cloned.1.call-start = ((), (), s32[]{:S(2)}) async-start(), calls=%async_computation.3 | async-start | bytes 56623104 | tf_op jit(solution)/shard_map/psum | solution.py:231
  301.0 2.9 copy-start.58
  303.9 18.8 %copy-start.36 = (f32[768]{0:T(1024)S(1)}, f32[768]{0:T(1024)}, u32[]{:S(2)}) copy-start(f32[768]{0:T(1024)} %param.30) | copy-start | bytes 9220
  322.8 11.0 %copy-start.42 = (f32[1024]{0:T(1024)S(1)}, f32[1024]{0:T(1024)}, u32[]{:S(2)}) copy-start(f32[1024]{0:T(1024)} %copy-done.41) | copy-start | bytes 12292
  322.8 11.0 %copy-start.5 = (f32[1024,768]{1,0:T(8,128)S(1)}, f32[1024,768]{1,0:T(8,128)}, u32[]{:S(2)}) copy-start(f32[1024,768]{1,0:T(8,128)} %copy-done.4) | copy-start | bytes 9437188
  339.5 6.6 copy-start.14
  339.5 6.6 copy-start.17
  339.5 6.6 copy-start.29
  377.2 21.9 %copy-start.11 = (bf16[2,512,12,64]{1,0,3,2:T(2,128)(2,1)S(1)}, bf16[2,512,12,64]{1,0,3,2:T(2,128)(2,1)}, u32[]{:S(2)}) copy-start(bf16[2,512,12,64]{1,0,3,2:T(2,128)(2,1)} %copy-done.10) | copy-start | bytes 4718596
  394.6 4.5 copy-start.1
  401.3 9.8 %copy-start.8 = (f32[1024,768]{1,0:T(8,128)S(1)}, f32[1024,768]{1,0:T(8,128)}, u32[]{:S(2)}) copy-start(f32[1024,768]{1,0:T(8,128)} %copy-done.7) | copy-start | bytes 9437188
  411.1 4.5 copy-start.6
  411.1 4.5 copy-start.40
  411.1 15.4 %slice-start.7 = ((s8[6291456]{0:T(1024)(128)(4,1)}), s8[4194304]{0:T(1024)(128)(4,1)S(1)}, s32[]{:S(2)}) async-start(s8[6291456]{0:T(1024)(128)(4,1)} %bitcast.117), calls=%async_computation.11 | async-start | bytes 8388608
  415.6 10.9 %copy-start.15 = (f32[1024,768]{1,0:T(8,128)S(1)}, f32[1024,768]{1,0:T(8,128)}, u32[]{:S(2)}) copy-start(f32[1024,768]{1,0:T(8,128)} %get-tuple-element.79) | copy-start | bytes 9437188
  415.6 10.9 %slice-start.8 = ((s8[6291456]{0:T(1024)(128)(4,1)}), s8[2097152]{0:T(1024)(128)(4,1)S(1)}, s32[]{:S(2)}) async-start(s8[6291456]{0:T(1024)(128)(4,1)} %bitcast.117), calls=%async_computation.12 | async-start | bytes 4194304
  426.5 8.2 copy-start.19
  436.8 7.4 copy-start.23
  450.0 3.4 copy-start.46
  450.0 3.4 copy-start.47
  497.1 3.4 copy-start.25
  497.1 3.4 copy-start.56
  880.4 3.2 copy-start.21
  885.5 3.2 copy-start.20
  888.7 10.7 %slice-start = ((s8[9437184]{0:T(1024)(128)(4,1)}), s8[4194304]{0:T(1024)(128)(4,1)S(1)}, s32[]{:S(2)}) async-start(s8[9437184]{0:T(1024)(128)(4,1)} %bitcast.98), calls=%async_computation.4 | async-start | bytes 8388608
  890.1 9.3 %slice-start.1 = ((s8[9437184]{0:T(1024)(128)(4,1)}), s8[4194304]{0:T(1024)(128)(4,1)S(1)}, s32[]{:S(2)}) async-start(s8[9437184]{0:T(1024)(128)(4,1)} %bitcast.98), calls=%async_computation.5 | async-start | bytes 8388608
  890.1 9.3 %slice-start.2 = ((s8[9437184]{0:T(1024)(128)(4,1)}), s8[1048576]{0:T(1024)(128)(4,1)S(1)}, s32[]{:S(2)}) async-start(s8[9437184]{0:T(1024)(128)(4,1)} %bitcast.98), calls=%async_computation.6 | async-start | bytes 2097152
  (27 other events, 55.6 us)
Sparse Core Ops, SparseCore 0:
  123.1 57.5 all-gather.1
  199.0 96.8 reduce-scatter.1
  450.0 430.3 all-reduce.3
where the time goes:
time: 920 us; the launch traced here: 910 us
  waiting for transfers between devices  526 us (57%)
  matrix products  204 us (22%)
  local copies, waits for them, and re-layouts  67.1 us (7%)
  other arithmetic  53.4 us (6%)
  blocking collectives  43.7 us (5%)
  between operations  15.1 us (2%)
    psum x1, waiting for transfers between devices, local(): lax.psum((dquery_weight, dquery_bias, dkey_weight, dvalue_weight, dvalue_...  374 us
    reduce_scatter x1, waiting for transfers between devices, local(): lax.psum_scatter(dense, ('dp', 'bucket'), scatter_dimension=0, tiled=True)  96.8 us
    all_gather x1, waiting for transfers between devices, local(): pooled_every = lax.all_gather(pooled, ('dp', 'bucket'), axis=0, tiled=True)  55.9 us
    dot_general x6, matrix products, matmul(): return jnp.dot(left, right, preferred_element_type=jnp.float32)  54.3 us
    psum x1, blocking collectives, local(): loss_value = lax.psum(jnp.sum(log_sum[:, 0] - diagonal), ('dp', 'bucket'))  43.7 us
    dot_general x6, matrix products, matmul_right(): lax.dot_general(left, right, (((1,), (1,)), ((), ())), preferred_element_...  40.8 us
    unnamed x154, local copies, waits for them, and re-layouts  34.3 us
    dot_general x6, matrix products, matmul_left(): lax.dot_general(left, right, (((0,), (0,)), ((), ())), preferred_element_...  31.9 us
  transfers between devices with their start and end apart: 3, of which 3 were waited for; matrix products, arithmetic and copies ran while one was open for 1% of the time, Pallas kernels for 0%

commit v1 on v0

--- a/solution.py
+++ b/solution.py
@@ -1,12 +1,17 @@
+import functools
+
 import jax
 import jax.numpy as jnp
 from jax import lax
+from jax.experimental import pallas as pl
+from jax.experimental.pallas import tpu as pltpu
 from jax.sharding import PartitionSpec as P
 
 H = 12
 HD = 64
 S_ROW = 8
 
+MESH = pl.DeviceIdType.MESH
 
 norm_eps = 1e-05
 cos_scale = 20.0
@@ -68,7 +73,192 @@
     return top + jnp.log(jnp.sum(jnp.exp(logits - top), axis=1, keepdims=True))
 
 
+def bit_dims(dp_size, bucket_size):
+    dims = []
+    for axis, size in ((1, bucket_size), (0, dp_size)):
+        bit = 1
+        while bit < size:
+            dims.append((axis, bit))
+            bit *= 2
+    return dims
+
+class Route:
+    def __init__(self, dims):
+        self.dims = dims
+        self.pos = (lax.axis_index("dp"), lax.axis_index("bucket"))
+        self.bits = [(self.pos[a] // b) % 2 for a, b in dims]
+
+    def weights(self, stage, colour=0):
+        core = self.bits[0]
+        n = len(self.dims)
+        if stage == 0 or n < 3:
+            return {stage: 1}
+        if n != 5 or isinstance(colour, int):
+            if stage in (1, 2):
+                return {stage: 1 - core, 3 - stage: core}
+            return {stage: 1}
+        keep = 1 - colour
+        table = {
+            1: {1: keep * (1 - core), 2: keep * core, 3: colour},
+            2: {2: keep * (1 - core), 1: keep * core, 4: colour},
+            3: {3: keep, 1: colour * (1 - core), 2: colour * core},
+            4: {4: keep, 2: colour * (1 - core), 1: colour * core},
+        }
+        return table[stage]
+
+    def bit(self, stage, colour=0):
+        w = self.weights(stage, colour)
+        return sum(v * self.bits[k] for k, v in w.items())
+
+    def partner(self, stage, colour=0):
+        where = list(self.pos)
+        for k, v in self.weights(stage, colour).items():
+            axis, bit = self.dims[k]
+            where[axis] = where[axis] + v * (bit * (1 - 2 * self.bits[k]))
+        return tuple(where)
+
+def colour_of(c):
+    return 1 - ((2 * c) % 9 + 7) // 9
+
+def ar_kernel(dims, nblk, colours, *refs):
+    ins = refs[:6]
+    vec_in, out, vec_out, grads = refs[6:10]
+    S = len(dims)
+    stages = refs[10:10 + S]
+    vbuf, vrecv, isem, ssem, rsem, osem, vs, vr, freed = refs[10 + S:]
+    blk = grads.shape[1]
+    rows = grads.shape[0]
+    CH = 8 << S
+    C = rows // CH
+    width = grads.shape[1]
+    route = Route(dims)
+    bar = pltpu.get_barrier_semaphore()
+    for k in range(S):
+        axis, bit = dims[k]
+        where = list(route.pos)
+        where[axis] = where[axis] + bit * (1 - 2 * route.bits[k])
+        pl.semaphore_signal(bar, inc=1, device_id=tuple(where), device_id_type=MESH)
+    srcs = []
+    for r in ins:
+        h, w = r.shape
+        for i in range(h // blk):
+            for j in range(w // width):
+                srcs.append(r.at[pl.ds(i * blk, blk), pl.ds(j * width, width)])
+    for b, s in enumerate(srcs):
+        pltpu.make_async_copy(s, grads.at[pl.ds(b * blk, blk)], isem.at[b]).start()
+    vbuf[0] = vec_in[...]
+    pl.semaphore_wait(bar, S)
+
+    def col(c):
+        return colour_of(c) if colours else 0
+    def base(s, c):
+        o = c * CH
+        for k in range(s):
+            o = o + route.bit(k, col(c)) * (CH >> (k + 1))
+        return o
+    def rs(s, c):
+        half = CH >> (s + 1)
+        b = route.bit(s, col(c))
+        o = base(s, c)
+        keep = pl.multiple_of(o + b * half, 8)
+        send = pl.multiple_of(o + (1 - b) * half, 8)
+        land = pl.multiple_of(c * half, 8)
+        cp = pltpu.make_async_remote_copy(grads.at[pl.ds(send, half)], stages[s].at[pl.ds(land, half)],
+            ssem.at[s, c], rsem.at[s, c], device_id=route.partner(s, col(c)), device_id_type=MESH)
+        return cp, keep, land, half
+    def ag(s, c):
+        half = CH >> (s + 1)
+        keep = pl.multiple_of(base(s, c) + route.bit(s, col(c)) * half, 8)
+        return pltpu.make_async_remote_copy(grads.at[pl.ds(keep, half)], grads.at[pl.ds(keep, half)],
+            ssem.at[2 * S - 1 - s, c], rsem.at[2 * S - 1 - s, c], device_id=route.partner(s, col(c)), device_id_type=MESH)
+    def outc(c):
+        o = pl.multiple_of(c * CH, 8)
+        return pltpu.make_async_copy(grads.at[pl.ds(o, CH)], out.at[pl.ds(o, CH)], osem.at[c])
+    def need(c):
+        return ((c + 1) * CH + blk - 1) // blk
+    def start(p, c):
+        if p == 0:
+            def w(b, _):
+                pltpu.make_async_copy(srcs[0], grads.at[pl.ds(pl.multiple_of(b * blk, 8), blk)], isem.at[b]).wait()
+                return 0
+            lo = need(c - 1)
+            lax.fori_loop(lo, need(c), w, 0)
+        if p < S:
+            rs(p, c)[0].start()
+        elif p < 2 * S:
+            pl.semaphore_wait(freed.at[2 * S - 1 - p, c], 1)
+            ag(2 * S - 1 - p, c).start()
+        else:
+            outc(c).start()
+    def finish(p, c):
+        if p < S:
+            cp, keep, land, half = rs(p, c)
+            cp.wait_recv()
+            grads[pl.ds(keep, half)] = grads[pl.ds(keep, half)] + stages[p][pl.ds(land, half)]
+            cp.wait_send()
+            pl.semaphore_signal(freed.at[p, c], inc=1, device_id=route.partner(p, col(c)), device_id_type=MESH)
+        elif p < 2 * S:
+            ag(2 * S - 1 - p, c).wait()
+        else:
+            outc(c).wait()
+    def vcopy(r):
+        axis, bit = dims[r]
+        where = list(route.pos)
+        where[axis] = where[axis] + bit * (1 - 2 * route.bits[r])
+        return pltpu.make_async_remote_copy(vbuf.at[r], vrecv.at[r], vs.at[r], vr.at[r], device_id=tuple(where), device_id_type=MESH)
+    NP = 2 * S + 1
+    def step(t, _):
+        for p in range(NP):
+            c = t - 2 * p
+            @pl.when((c >= 0) & (c < C))
+            def _():
+                start(p, c)
+        for r in range(S):
+            @pl.when(t == 2 + 2 * r)
+            def _():
+                vcopy(r).start()
+        for p in range(NP):
+            c = t - 1 - 2 * p
+            @pl.when((c >= 0) & (c < C))
+            def _():
+                finish(p, c)
+        for r in range(S):
+            @pl.when(t == 3 + 2 * r)
+            def _():
+                cp = vcopy(r)
+                cp.wait()
+                vbuf[r + 1] = vbuf[r] + vrecv[r]
+        return 0
+    lax.fori_loop(0, C + 2 * (NP - 1) + 1, step, 0)
+    vec_out[...] = vbuf[S]
+
+def all_reduce(parts, vec, dp_size, bucket_size, colours=False):
+    dims = bit_dims(dp_size, bucket_size)
+    S = len(dims)
+    width = parts[0].shape[1]
+    rows = sum(p.size for p in parts) // width
+    nblk = rows // width
+    CH = 8 << S
+    f32 = jnp.float32
+    any_spec = pl.BlockSpec(memory_space=pl.ANY)
+    vm = pl.BlockSpec(memory_space=pltpu.VMEM)
+    return pl.pallas_call(
+        functools.partial(ar_kernel, dims, nblk, colours),
+        out_shape=(jax.ShapeDtypeStruct((rows, width), f32), jax.ShapeDtypeStruct(vec.shape, f32)),
+        in_specs=[any_spec] * 6 + [vm], out_specs=(any_spec, vm),
+        scratch_shapes=[pltpu.VMEM((rows, width), f32)]
+        + [pltpu.VMEM((rows >> (s + 1), width), f32) for s in range(S)]
+        + [pltpu.VMEM((S + 1,) + vec.shape, f32), pltpu.VMEM((S,) + vec.shape, f32),
+           pltpu.SemaphoreType.DMA((nblk,)), pltpu.SemaphoreType.DMA((2 * S, rows // CH)), pltpu.SemaphoreType.DMA((2 * S, rows // CH)),
+           pltpu.SemaphoreType.DMA((rows // CH,)), pltpu.SemaphoreType.DMA((S,)), pltpu.SemaphoreType.DMA((S,)),
+           pltpu.SemaphoreType.REGULAR((S, rows // CH))],
+        compiler_params=pltpu.CompilerParams(collective_id=1, has_side_effects=True, vmem_limit_bytes=67043328),
+    )(*parts, vec)
+
+
 def local(
+    dp_size,
+    bucket_size,
     tokens,
     segment,
     pair_order,
@@ -132,27 +322,23 @@
     sents = pooled_every.shape[0]
     pairs = sents // 2
     device = lax.axis_index(("dp", "bucket"))
-    ordered = pooled_every[pair_order]
-    unit_p, factor_p = to_sphere(ordered[pairs:])
-    share = pairs // lax.axis_size(("dp", "bucket"))
-    first_pair = device * share
-    unit_a, factor_a = to_sphere(lax.dynamic_slice_in_dim(ordered, first_pair, share, 0))
+    unit, factor = to_sphere(pooled_every[pair_order])
+    unit_a, unit_p = unit[:pairs], unit[pairs:]
     logits = cos_scale * exact_dot(unit_a, unit_p, ((1,), (1,)))
     log_sum = row_logsum(logits)
-    diagonal = jnp.diagonal(lax.dynamic_slice_in_dim(logits, first_pair, share, 1))
-    loss_value = lax.psum(jnp.sum(log_sum[:, 0] - diagonal), ("dp", "bucket"))
     columns = jnp.arange(pairs, dtype=jnp.int32)[None, :]
-    targets = (first_pair + jnp.arange(share, dtype=jnp.int32))[:, None]
-    weighting = jnp.exp(logits - log_sum) - (columns == targets).astype(jnp.float32)
-    grad_anchor = sphere_back(
-        unit_a, factor_a, cos_scale * exact_dot(weighting, unit_p, ((1,), (0,)))
-    )
-    grad_positive = sphere_back(
-        unit_p, factor_p, cos_scale * exact_dot(weighting, unit_a, ((0,), (0,)))
-    )
-    dense = jnp.zeros((sents, width), jnp.float32).at[pair_order[pairs:]].set(grad_positive)
-    dense = dense.at[lax.dynamic_slice_in_dim(pair_order, first_pair, share, 0)].set(grad_anchor)
-    dpooled = lax.psum_scatter(dense, ("dp", "bucket"), scatter_dimension=0, tiled=True)
+    on_diagonal = (columns == columns.T).astype(jnp.float32)
+    loss_value = jnp.sum(log_sum[:, 0] - jnp.sum(logits * on_diagonal, axis=1))
+    weighting = jnp.exp(logits - log_sum) - on_diagonal
+    mine = device * nrows * S_ROW + jnp.arange(nrows * S_ROW, dtype=jnp.int32)
+    pick = (mine[:, None] == pair_order[None, :]).astype(jnp.float32)
+    row_part = exact_dot(pick[:, :pairs], weighting, ((1,), (0,)))
+    column_part = exact_dot(pick[:, pairs:], weighting, ((1,), (1,)))
+    grad_unit = cos_scale * (
+        exact_dot(row_part, unit_p, ((1,), (0,))) + exact_dot(column_part, unit_a, ((1,), (0,)))
+    )
+    unit_own, factor_own = to_sphere(pooled)
+    dpooled = sphere_back(unit_own, factor_own, grad_unit)
     spread_back = jnp.einsum(
         "rsl,rsd->rld",
         onehot,
@@ -212,42 +398,29 @@
         + matmul_right(grad_key_b, key_weight)
         + matmul_right(grad_value_b, value_weight)
     )
+    vectors = [
+        dquery_bias, dvalue_bias, dout_bias, dnorm_gain, dnorm_shift,
+        dinner_bias, douter_bias, dfinal_gain, dfinal_shift,
+    ]
+    packed = jnp.concatenate(vectors).reshape(-1, width)
+    nvec = packed.shape[0]
+    packed = jnp.pad(packed, ((0, -nvec % 8), (0, 0)))
+    flat, packed = all_reduce(
+        [douter_weight, dinner_weight, dout_weight, dquery_weight, dkey_weight, dvalue_weight],
+        packed, dp_size, bucket_size,
+    )
+    blocks = flat.reshape(-1, width, width)
+    wide = inner_weight.shape[1] // width
+    douter_weight = flat[: wide * width]
+    dinner_weight = jnp.concatenate([blocks[wide + j] for j in range(wide)], axis=1)
+    dout_weight, dquery_weight, dkey_weight, dvalue_weight = (blocks[2 * wide + j] for j in range(4))
+    packed = packed[:nvec].reshape(-1)
+    sizes = [v.shape[0] for v in vectors]
+    ends = [sum(sizes[: i + 1]) for i in range(len(sizes))]
     (
-        dquery_weight,
-        dquery_bias,
-        dkey_weight,
-        dvalue_weight,
-        dvalue_bias,
-        dout_weight,
-        dout_bias,
-        dnorm_gain,
-        dnorm_shift,
-        dinner_weight,
-        dinner_bias,
-        douter_weight,
-        douter_bias,
-        dfinal_gain,
-        dfinal_shift,
-    ) = lax.psum(
-        (
-            dquery_weight,
-            dquery_bias,
-            dkey_weight,
-            dvalue_weight,
-            dvalue_bias,
-            dout_weight,
-            dout_bias,
-            dnorm_gain,
-            dnorm_shift,
-            dinner_weight,
-            dinner_bias,
-            douter_weight,
-            douter_bias,
-            dfinal_gain,
-            dfinal_shift,
-        ),
-        ("dp", "bucket"),
-    )
+        dquery_bias, dvalue_bias, dout_bias, dnorm_gain, dnorm_shift,
+        dinner_bias, douter_bias, dfinal_gain, dfinal_shift,
+    ) = (packed[e - n : e] for e, n in zip(ends, sizes))
     return (
         layer_out,
         loss_value,
@@ -272,7 +445,7 @@
 
 def solution(mesh):
     return jax.shard_map(
-        local,
+        functools.partial(local, mesh.shape["dp"], mesh.shape["bucket"]),
         mesh=mesh,
         in_specs=(
             P(("dp", "bucket"), None),

time: 920 us -> 659 us (0.72)
  waiting for transfers between devices: 526 us -> 57.5 us
  Pallas kernels: 0 us -> 249 us
  blocking collectives: 43.7 us -> 0 us
    psum x1 -> x0, waiting for transfers between devices: 374 us -> none  [local(): lax.psum((dquery_weight, dquery_bias, dkey_weight, dvalue_weight, dvalue_...]
    pallas_call x0 -> x1, Pallas kernels: none -> 249 us  [all_reduce(): pl.pallas_call(functools.partial(ar_kernel, dims, nblk, colours), out_sha...]
    reduce_scatter x1 -> x0, waiting for transfers between devices: 96.8 us -> none  [local(): lax.psum_scatter(dense, ('dp', 'bucket'), scatter_dimension=0, tiled=True)]
    psum x1 -> x0, blocking collectives: 43.7 us -> none  [local(): loss_value = lax.psum(jnp.sum(log_sum[:, 0] - diagonal), ('dp', 'bucket'))]
    unnamed x154 -> x124, local copies, waits for them, and re-layouts: 34.3 us -> 9.16 us
    slice x0 -> x5, local copies, waits for them, and re-layouts: none -> 24.6 us  [the longest x1 13.4 us: local(): blocks[wide + j]]
  transfers between devices with their start and end apart: 3 -> 1, of which waited for: 3 -> 1; matrix products, arithmetic and copies ran while one was open for 1% -> 0% of each run, Pallas kernels for 0% -> 0%
where the time goes in v1:
time: 659 us; the launch traced here: 649 us
  Pallas kernels  249 us (38%)
  matrix products  212 us (32%)
  local copies, waits for them, and re-layouts  61.9 us (9%)
  waiting for transfers between devices  57.5 us (9%)
  other arithmetic  54.5 us (8%)
  between operations  15.1 us (2%)
    pallas_call x1, Pallas kernels, all_reduce(): pl.pallas_call(functools.partial(ar_kernel, dims, nblk, colours), out_sha...  249 us
    all_gather x1, waiting for transfers between devices, local(): pooled_every = lax.all_gather(pooled, ('dp', 'bucket'), axis=0, tiled=True)  57.5 us
    dot_general x6, matrix products, matmul(): return jnp.dot(left, right, preferred_element_type=jnp.float32)  51.8 us
    dot_general x6, matrix products, matmul_right(): lax.dot_general(left, right, (((1,), (1,)), ((), ())), preferred_element_...  45.2 us
    dot_general x6, matrix products, matmul_left(): lax.dot_general(left, right, (((0,), (0,)), ((), ())), preferred_element_...  33.4 us
    convert_element_type x1, other arithmetic, local(): grad_scores_b = grad_scores.astype(jnp.bfloat16)  21.4 us
    dot_general x1, matrix products, local(): jnp.einsum('rqhe,rkhe->rhqk', grad_context, value_h, preferred_element_ty...  21.2 us
    slice x1, local copies, waits for them, and re-layouts, local(): blocks[wide + j]  13.4 us
  transfers between devices with their start and end apart: 1, of which 1 were waited for; matrix products, arithmetic and copies ran while one was open for 0% of the time, Pallas kernels for 0%

profile of v1, /device:TPU:0, one launch (start us, length us, event | category | flops | bytes accessed | tf_op | source)
XLA Modules:
  0.0 649.3 jit_solution(5220483239904490718)
XLA Ops:
  7.2 1.9 broadcast_compare_fusion
  9.9 3.2 add_convert_fusion.1
  13.9 2.4 reshape.224
  16.2 2.7 convolution_convert_fusion.2
  20.9 3.7 add_convert_fusion
  24.6 1.6 copy.53
  26.2 2.9 reshape.225
  29.1 11.6 %fusion = (f32[2,12,512]{2,1,0:T(8,128)S(1)}, f32[2,12,512,512]{2,3,1,0:T(8,128)}) fusion(pred[2,512,512]{1,2,0:T(8,128)(4,1)} %broadcast_compare_fusion, bf16[2,512,12,64]{1,0,3,2:T(2,128)(2,1)S(1)} %reshape.226, bf16[2,512,12,64]{1,0,3,2:T(2,128)(2,1)S(1)} %reshape.225), kind=kOutput, calls=%fused_computation.6 | convolution fusion | flops 824168448 | bytes 28884992 | tf_op jit(solution)/shard_map/rqhe,rkhe->rhqk/dot_general | solution.py:67
  40.8 11.2 %exponential_reduce_fusion = f32[2,12,512]{2,1,0:T(8,128)S(1)} fusion(f32[2,12,512,512]{2,3,1,0:T(8,128)} %get-tuple-element.57, f32[2,12,512]{2,1,0:T(8,128)S(1)} %get-tuple-element.56, pred[2,512,512]{1,2,0:T(8,128)(4,1)S(1)} %copy-done.9), kind=kLoop, calls=%fused_computation.4 | loop fusion | flops 25153536 | bytes 25788416 | tf_op jit(solution)/shard_map/reduce_sum | solution.py:294
  52.0 11.9 %fusion.15 = bf16[2,512,12,64]{1,3,2,0:T(8,128)(2,1)S(1)} fusion(bf16[2,512,12,64]{1,0,3,2:T(2,128)(2,1)S(1)} %copy-done.16, f32[2,12,512,512]{2,3,1,0:T(8,128)} %get-tuple-element.57, f32[2,12,512]{2,1,0:T(8,128)S(1)} %log_add_fusion, pred[2,512,512]{1,2,0:T(8,128)(4,1)S(1)} %copy-done.9), kind=kOutput, calls=%fused_computation.64 | convolution fusion | flops 831258624 | bytes 28884992 | tf_op jit(solution)/shard_map/rhqk,rkhe->rqhe/dot_general | solution.py:296
  64.0 1.6 copy.59
  66.1 1.7 fusion.71
  70.5 35.2 %multiply_convert_fusion.1 = (bf16[1024,3072]{1,0:T(8,128)(2,1)S(1)}, f32[1024,3072]{1,0:T(8,128)}, f32[1024,3072]{1,0:T(8,128)}) fusion(f32[3072]{0:T(1024)S(1)} %copy-done.47, bf16[768,3072]{1,0:T(8,128)(2,1)S(1)} %bitcast.117, f32[1024,768]{1,0:T(8,128)S(1)} %get-tuple-element.59, f32[768]{0:T(1024)S(1)} %copy-done.30, f32[768]{0:T(1024)S(1)} %copy-done.28, ...), kind=kOutput, calls=%fused_computation.11 | convolution fusion | flops 5043388416 | bytes 39348224 | tf_op jit(solution)/shard_map/dot_general | solution.py:32
  105.8 5.4 fusion.72
  111.9 1.7 fusion.68
  113.7 1.8 multiply_reduce_fusion.9
  115.7 57.5 %all-gather.2.cloned.1.call-done = f32[512,768]{1,0:T(8,128)} async-done(((f32[16,768]{1,0:T(8,128)}), f32[512,768]{1,0:T(8,128)}) %all-gather.2.cloned.1.call-update) | async-done | bytes 1572880 | tf_op jit(solution)/shard_map/all_gather | solution.py:321
  173.2 4.6 gather_fusion
  185.6 2.5 multiply_reduce_fusion.1
  188.2 3.2 fusion.67
  191.4 19.0 %fusion.74 = (f32[3072]{0:T(1024)S(1)}, bf16[1024,3072]{1,0:T(8,128)(2,1)}) fusion(f32[1024,3072]{1,0:T(8,128)} %get-tuple-element.47, bf16[3072,768]{1,0:T(8,128)(2,1)} %param.34, f32[1024,768]{1,0:T(8,128)} %get-tuple-element.41, f32[1024]{0:T(1024)S(1)} %negate_multiply_fusion.2, f32[1024,3072]{1,0:T(8,128)} %get-tuple-element.60, f32[3072]{0:T(1024)S(1)} %copy-done.47), kind=kOutput, calls=%fused_computation.166 | convolution fusion | flops 4883739648 | bytes 39350272 | tf_op jit(solution)/shard_map/dot_general | solution.py:42
  210.4 10.0 %multiply_reduce_fusion.2 = (f32[768]{0:T(1024)S(1)}, f32[1024]{0:T(1024)S(1)}, f32[768]{0:T(1024)S(1)}, f32[1024,768]{1,0:T(8,128)S(1)}) fusion(f32[1024,768]{1,0:T(8,128)S(1)} %copy-done.1, f32[1024]{0:T(1024)S(1)} %fusion.54, f32[1024]{0:T(1024)S(1)} %broadcast_multiply_fusion.2, f32[768]{0:T(1024)S(1)} %copy-done.28, bf16[768,3072]{1,0:T(8,128)(2,1)} %param.32, ...), kind=kOutput, calls=%fused_computation.34 | convolution fusion | flops 4839699456 | bytes 20472832 | tf_op jit(solution)/shard_map/dot_general | solution.py:42
  221.9 1.7 copy-done.2
  223.6 2.6 convolution_convert_fusion.1
  226.2 2.6 copy.60
  228.8 3.8 reshape.232
  232.6 21.2 %multiply_reduce_fusion = (f32[2,12,512]{2,1,0:T(8,128)S(1)}, f32[2,12,512,512]{2,3,1,0:T(8,128)}) fusion(f32[2,12,512,512]{2,3,1,0:T(8,128)} %get-tuple-element.57, f32[2,12,512]{2,1,0:T(8,128)S(1)} %copy-done.26, pred[2,512,512]{1,2,0:T(8,128)(4,1)} %broadcast_compare_fusion, bf16[2,512,12,64]{1,0,3,2:T(2,128)(2,1)} %reshape.224, ...), kind=kOutput, calls=%fused_computation.2 | convolution fusion | flops 836751360 | bytes 54099968 | tf_op jit(solution)/shard_map/rqhe,rkhe->rhqk/dot_general | solution.py:368
  253.8 21.4 %multiply_convert_fusion = bf16[2,12,512,512]{2,3,1,0:T(8,128)(2,1)} fusion(f32[2,12,512,512]{2,3,1,0:T(8,128)} %get-tuple-element.71, f32[2,12,512,512]{2,3,1,0:T(8,128)} %get-tuple-element.57, f32[2,12,512]{2,1,0:T(8,128)S(1)} %get-tuple-element.70, f32[2,12,512]{2,1,0:T(8,128)S(1)} %copy-done.26, pred[2,512,512]{1,2,0:T(8,128)(4,1)} %broadcast_compare_fusion), kind=kLoop, calls=%fused_computation.1 | loop fusion | flops 37748736 | bytes 63537152 | tf_op jit(solution)/shard_map/convert_element_type | solution.py:375
  275.3 9.7 %fusion.16 = bf16[2,512,12,64]{1,3,2,0:T(8,128)(2,1)} fusion(bf16[2,12,512,512]{2,3,1,0:T(8,128)(2,1)} %multiply_convert_fusion, bf16[2,512,12,64]{1,0,3,2:T(2,128)(2,1)S(1)} %copy-done.8), kind=kOutput, calls=%fused_computation.65 | convolution fusion | flops 806879232 | bytes 15728640 | tf_op jit(solution)/shard_map/rhqk,rqhe->rkhe/dot_general | solution.py:381
  285.0 7.8 %bitcast_convert_fusion.1 = (bf16[2,512,12,64]{1,3,2,0:T(8,128)(2,1)}, f32[2,12,64,512]{3,2,1,0:T(8,128)S(1)}) fusion(bf16[2,12,512,512]{2,3,1,0:T(8,128)(2,1)} %multiply_convert_fusion, bf16[2,512,12,64]{1,0,3,2:T(2,128)(2,1)S(1)} %copy-done.6), kind=kOutput, calls=%fused_computation.31 | convolution fusion | flops 806879232 | bytes 18874368 | tf_op jit(solution)/shard_map/rhqk,rkhe->rqhe/dot_general | solution.py:377
  292.8 13.2 %bitcast_convert_fusion = (bf16[2,512,12,64]{1,3,2,0:T(8,128)(2,1)}, f32[2,12,64,512]{3,2,1,0:T(8,128)}) fusion(f32[2,12,512,512]{2,3,1,0:T(8,128)} %get-tuple-element.57, f32[2,12,512]{2,1,0:T(8,128)S(1)} %copy-done.26, pred[2,512,512]{1,2,0:T(8,128)(4,1)} %broadcast_compare_fusion, bf16[2,512,12,64]{1,0,3,2:T(2,128)(2,1)} %reshape.232), kind=kOutput, calls=%fused_computation.29 | convolution fusion | flops 831258624 | bytes 32030720 | tf_op jit(solution)/shard_map/rhqk,rqhe->rkhe/dot_general | solution.py:371
  306.1 10.6 %fusion.61.refs_0_ = f32[3072,768]{1,0:T(8,128)} fusion(bf16[1024,3072]{1,0:T(8,128)(2,1)} %copy-done.51, f32[1024,768]{1,0:T(8,128)} %get-tuple-element.41, f32[1024]{0:T(1024)S(1)} %negate_multiply_fusion.2), kind=kOutput, calls=%fused_computation.156 | convolution fusion | flops 4833411072 | bytes 18878464 | tf_op jit(solution)/shard_map/dot_general | solution.py:36
  316.6 11.2 %fusion.8.refs_1_ = f32[768,3072]{1,0:T(8,128)} fusion(bf16[1024,3072]{1,0:T(8,128)(2,1)} %get-tuple-element.77, f32[1024,768]{1,0:T(8,128)S(1)} %copy-done.1, f32[768]{0:T(1024)S(1)} %copy-done.30, f32[768]{0:T(1024)S(1)} %copy-done.28, f32[1024]{0:T(1024)S(1)} %fusion.54, f32[1024]{0:T(1024)S(1)} %broadcast_multiply_fusion.2), kind=kOutput, calls=%fused_computation.38 | convolution fusion | flops 4835770368 | bytes 18888704 | tf_op jit(solution)/shard_map/dot_general | solution.py:36
  327.9 2.9 fusion.62.refs_2_
  330.8 1.6 copy.65
  332.9 3.2 fusion.75
  336.1 2.9 convolution_bitcast_fusion.2.refs_3_
  339.0 1.6 copy.68
  341.0 3.1 fusion.76
  344.2 2.9 convolution_bitcast_fusion.1.refs_4_
  349.4 1.8 copy.71
  351.6 2.9 convolution_bitcast_fusion.refs_5_
  357.5 248.6 %shard_map.322 = (f32[9216,768]{1,0:T(8,128)}, f32[16,768]{1,0:T(8,128)}) custom-call(f32[3072,768]{1,0:T(8,128)} %fusion.61.refs_0_, f32[768,3072]{1,0:T(8,128)} %fusion.8.refs_1_, f32[768,768]{1,0:T(8,128)} %fusion.62.refs_2_, f32[768,768]{1,0:T(8,128)} %convolution_bitcast_fusion.2.refs_3_, f32[768,768]{1,0:T(8,128)} %convolution_bitcast_fusion.1.refs_4_, ...), custom_call_target="tpu_custom_call" | custom-call | tf_op jit(solution)/shard_map/pallas_call | solution.py:245
  606.1 1.6 slice_reduce_fusion
  608.5 13.4 %fusion.70 = (f32[768,768]{1,0:T(8,128)}, f32[768,768]{1,0:T(8,128)}, f32[768,768]{1,0:T(8,128)}, f32[768,768]{1,0:T(8,128)}, f32[768,768]{1,0:T(8,128)}, /*inde...) fusion(f32[9216,768]{1,0:T(8,128)} %get-tuple-element.20), kind=kLoop, calls=%fused_computation.162 | loop fusion | bytes 37748736 | tf_op jit(solution)/shard_map/slice | solution.py:415
  621.9 8.2 %slice.135 = f32[3072,768]{1,0:T(8,128)} slice(f32[9216,768]{1,0:T(8,128)} %get-tuple-element.20), slice={[0:3072], [0:768]} | slice | bytes 18874368 | tf_op jit(solution)/shard_map/slice | solution.py:414
  630.7 7.4 %add_add_fusion.2 = f32[1024,768]{1,0:T(8,128)} fusion(f32[1024,768]{1,0:T(8,128)} %fusion.76, f32[1024,768]{1,0:T(8,128)} %fusion.75, f32[1024,768]{1,0:T(8,128)S(1)} %copy-done.4, bf16[1024,768]{0,1:T(8,128)(2,1)} %bitcast.102, bf16[768,768]{1,0:T(8,128)(2,1)} %param.26, f32[1024]{0:T(1024)S(1)} %copy-done.32), kind=kOutput, calls=%fused_computation.35 | convolution fusion | flops 1211105280 | bytes 15339520 | tf_op jit(solution)/shard_map/dot_general | solution.py:42
  638.1 4.1 pad_maximum_fusion
  (172 shorter events, 24.8 us)
Async XLA Ops:
  7.2 166.0 %all-gather.2.cloned.1.call-start = ((), (), s32[]{:S(2)}) async-start(), calls=%async_computation | async-start | bytes 1622016 | tf_op jit(solution)/shard_map/all_gather | solution.py:321
  13.9 2.4 copy-start.40
  20.9 8.2 %copy-start.5 = (bf16[2,512,12,64]{1,0,3,2:T(2,128)(2,1)}, bf16[2,512,12,64]{1,0,3,2:T(2,128)(2,1)S(1)}, u32[]{:S(2)}) copy-start(bf16[2,512,12,64]{1,0,3,2:T(2,128)(2,1)S(1)} %reshape.226) | copy-start | bytes 4718596
  29.1 11.7 %copy-start.7 = (bf16[2,512,12,64]{1,0,3,2:T(2,128)(2,1)}, bf16[2,512,12,64]{1,0,3,2:T(2,128)(2,1)S(1)}, u32[]{:S(2)}) copy-start(bf16[2,512,12,64]{1,0,3,2:T(2,128)(2,1)S(1)} %reshape.225) | copy-start | bytes 4718596
  29.1 11.7 %copy-start.9 = (pred[2,512,512]{1,2,0:T(8,128)(4,1)S(1)}, pred[2,512,512]{1,2,0:T(8,128)(4,1)}, u32[]{:S(2)}) copy-start(pred[2,512,512]{1,2,0:T(8,128)(4,1)} %broadcast_compare_fusion) | copy-start | bytes 1572868
  40.8 11.2 %copy-start.16 = (bf16[2,512,12,64]{1,0,3,2:T(2,128)(2,1)S(1)}, bf16[2,512,12,64]{1,0,3,2:T(2,128)(2,1)}, u32[]{:S(2)}) copy-start(bf16[2,512,12,64]{1,0,3,2:T(2,128)(2,1)} %reshape.224) | copy-start | bytes 4718596
  52.0 11.9 %copy-start.25 = (f32[2,12,512]{2,1,0:T(8,128)}, f32[2,12,512]{2,1,0:T(8,128)S(1)}, u32[]{:S(2)}) copy-start(f32[2,12,512]{2,1,0:T(8,128)S(1)} %log_add_fusion) | copy-start | bytes 147460
  64.0 2.1 copy-start.41
  64.0 2.1 copy-start.43
  64.0 2.1 copy-start.49
  66.0 2.9 slice-start.2
  66.1 3.4 slice-start.3
  66.1 39.6 %slice-start = ((s8[4718592]{0:T(1024)(128)(4,1)}), s8[4194304]{0:T(1024)(128)(4,1)S(1)}, s32[]{:S(2)}) async-start(s8[4718592]{0:T(1024)(128)(4,1)} %bitcast.114), calls=%async_computation.1 | async-start | bytes 8388608
  67.8 37.9 %copy-start = (f32[1024,768]{1,0:T(8,128)}, f32[1024,768]{1,0:T(8,128)S(1)}, u32[]{:S(2)}) copy-start(f32[1024,768]{1,0:T(8,128)S(1)} %get-tuple-element.59) | copy-start | bytes 9437188
  67.8 2.6 copy-start.28
  67.8 2.6 copy-start.30
  67.8 2.6 copy-start.47
  68.4 37.3 %copy-start.33 = (f32[1024]{0:T(1024)}, f32[1024]{0:T(1024)S(1)}, u32[]{:S(2)}) copy-start(f32[1024]{0:T(1024)S(1)} %multiply_reduce_fusion.6) | copy-start | bytes 12292
  70.5 35.3 %slice-start.1 = ((s8[4718592]{0:T(1024)(128)(4,1)}), s8[524288]{0:T(1024)(128)(4,1)S(1)}, s32[]{:S(2)}) async-start(s8[4718592]{0:T(1024)(128)(4,1)} %bitcast.114), calls=%async_computation.2 | async-start | bytes 1048576
  70.5 35.3 %copy-start.50 = (f32[768]{0:T(1024)S(1)}, f32[768]{0:T(1024)}, u32[]{:S(2)}) copy-start(f32[768]{0:T(1024)} %param.35) | copy-start | bytes 9220
  105.7 5.5 copy-start.51
  179.3 4.2 copy-start.24
  181.8 3.8 copy-start.17
  191.4 19.0 %copy-start.1 = (f32[1024,768]{1,0:T(8,128)S(1)}, f32[1024,768]{1,0:T(8,128)}, u32[]{:S(2)}) copy-start(f32[1024,768]{1,0:T(8,128)} %copy-done) | copy-start | bytes 9437188
  210.4 10.0 %copy-start.34 = (f32[1024]{0:T(1024)S(1)}, f32[1024]{0:T(1024)}, u32[]{:S(2)}) copy-start(f32[1024]{0:T(1024)} %copy-done.33) | copy-start | bytes 12292
  220.4 3.2 copy-start.44
  221.9 125.2 %copy-start.31 = (f32[1024]{0:T(1024)}, f32[1024]{0:T(1024)S(1)}, u32[]{:S(2)}) copy-start(f32[1024]{0:T(1024)S(1)} %negate_multiply_fusion.1) | copy-start | bytes 12292
  226.2 6.5 copy-start.26
  253.8 21.4 %copy-start.8 = (bf16[2,512,12,64]{1,0,3,2:T(2,128)(2,1)S(1)}, bf16[2,512,12,64]{1,0,3,2:T(2,128)(2,1)}, u32[]{:S(2)}) copy-start(bf16[2,512,12,64]{1,0,3,2:T(2,128)(2,1)} %copy-done.7) | copy-start | bytes 4718596
  275.3 9.7 %copy-start.6 = (bf16[2,512,12,64]{1,0,3,2:T(2,128)(2,1)S(1)}, bf16[2,512,12,64]{1,0,3,2:T(2,128)(2,1)}, u32[]{:S(2)}) copy-start(bf16[2,512,12,64]{1,0,3,2:T(2,128)(2,1)} %copy-done.5) | copy-start | bytes 4718596
  316.6 11.2 %copy-start.3 = (f32[1024,768]{1,0:T(8,128)S(1)}, f32[1024,768]{1,0:T(8,128)}, u32[]{:S(2)}) copy-start(f32[1024,768]{1,0:T(8,128)} %copy-done.2) | copy-start | bytes 9437188
  316.6 11.2 %copy-start.22 = (bf16[96,8,2,512]{3,1,2,0:T(8,128)(2,1)S(1)}, bf16[96,8,2,512]{3,1,2,0:T(8,128)(2,1)}, u32[]{:S(2)}) copy-start(bf16[96,8,2,512]{3,1,2,0:T(8,128)(2,1)} %copy-done.21) | copy-start | bytes 4718596
  327.9 2.9 copy-start.11
  330.8 2.0 copy-start.45
  332.9 3.2 copy-start.42
  336.1 2.9 copy-start.19
  339.0 2.0 copy-start.46
  347.0 2.4 copy-start.23
  351.6 2.9 copy-start.18
  354.5 2.2 copy-start.35
  354.5 2.3 copy-start.37
  354.5 2.3 copy-start.36
  621.9 8.8 %copy-start.4 = (f32[1024,768]{1,0:T(8,128)S(1)}, f32[1024,768]{1,0:T(8,128)}, u32[]{:S(2)}) copy-start(f32[1024,768]{1,0:T(8,128)} %copy-done.2) | copy-start | bytes 9437188
  621.9 8.8 %copy-start.32 = (f32[1024]{0:T(1024)S(1)}, f32[1024]{0:T(1024)}, u32[]{:S(2)}) copy-start(f32[1024]{0:T(1024)} %copy-done.31) | copy-start | bytes 12292
  630.7 7.4 %copy-start.12 = (f32[768,768]{1,0:T(8,128)S(1)}, f32[768,768]{1,0:T(8,128)}, u32[]{:S(2)}) copy-start(f32[768,768]{1,0:T(8,128)} %get-tuple-element.48) | copy-start | bytes 7077892
  630.7 7.4 %copy-start.13 = (f32[768,768]{1,0:T(8,128)S(1)}, f32[768,768]{1,0:T(8,128)}, u32[]{:S(2)}) copy-start(f32[768,768]{1,0:T(8,128)} %get-tuple-element.49) | copy-start | bytes 7077892
  630.7 7.4 %copy-start.14 = (f32[768,768]{1,0:T(8,128)S(1)}, f32[768,768]{1,0:T(8,128)}, u32[]{:S(2)}) copy-start(f32[768,768]{1,0:T(8,128)} %get-tuple-element.50) | copy-start | bytes 7077892
  630.7 7.4 %copy-start.15 = (f32[768,768]{1,0:T(8,128)S(1)}, f32[768,768]{1,0:T(8,128)}, u32[]{:S(2)}) copy-start(f32[768,768]{1,0:T(8,128)} %get-tuple-element.51) | copy-start | bytes 7077892
  (9 other events, 14.3 us)
Sparse Core Ops, SparseCore 0:
  115.6 57.5 all-gather.1

commit v2 on v1

v2 whole, which is shorter than its diff:
```python
import functools

import jax
import jax.numpy as jnp
import numpy as np
from jax import lax
from jax.experimental import pallas as pl
from jax.experimental.pallas import tpu as pltpu
from jax.sharding import PartitionSpec as P

H = 12
HD = 64
S_ROW = 8
norm_eps = 1e-05
masked_score = -1000000000.0
BF = jnp.bfloat16
F32 = jnp.float32
HIGH = lax.Precision.HIGHEST


def dot(a, b, da, db, precision=None):
    return lax.dot_general(
        a, b, (((da,), (db,)), ((), ())), precision=precision, preferred_element_type=F32
    )


def halves(width=128):
    lane = lax.broadcasted_iota(jnp.int32, (1, width), 1)
    low = (lane < width // 2).astype(F32)
    return low.astype(BF), (1.0 - low).astype(BF)


def normalise(hidden):
    centred = hidden - jnp.mean(hidden, axis=-1, keepdims=True)
    rate = lax.rsqrt(jnp.mean(centred * centred, axis=-1, keepdims=True) + norm_eps)
    return centred * rate, rate


def forward_kernel(
    x_in, seg_row, seg_col, wq_h, bq, wk_h, wv_h, bv, wo_h, bo, g1, s1, wi_h, bi, w2_h, b2, g2, s2,
    q_o, k_o, v_o, c_o, nb_o, z1_o, r1_o, act_o, dg_o, z2_o, r2_o, lse_o, out_o, pool_o,
    wq, wk, wv, wo, wi, w2, q, k, v, ctx, nf, nb, z1, r1, act, dg, z2, r2, fin, lout, bias,
    wsem, osem,
):
    rows, width = x_in.shape
    nrow = seg_row.shape[0]
    seqlen = rows // nrow
    pairs = width // 128
    inner = wi.shape[1]
    TM = 256
    loads = [
        pltpu.make_async_copy(a, b, wsem.at[i])
        for i, (a, b) in enumerate(
            [(wq_h, wq), (wk_h, wk), (wv_h, wv), (wo_h, wo), (wi_h, wi), (w2_h, w2)]
        )
    ]
    for c in loads:
        c.start()
    stores = []

    def put(i, src, dst):
        c = pltpu.make_async_copy(src, dst, osem.at[i])
        c.start()
        stores.append(c)

    def tile(i):
        return pl.ds(pl.multiple_of(i * TM, TM), TM)

    for c in loads[:3]:
        c.wait()

    def project(i, _):
        x = x_in[tile(i)]
        q[tile(i)] = (dot(x, wq[...], 1, 0) + bq[...]).astype(BF)
        k[tile(i)] = dot(x, wk[...], 1, 0).astype(BF)
        v[tile(i)] = (dot(x, wv[...], 1, 0) + bv[...]).astype(BF)
        return 0

    lax.fori_loop(0, rows // TM, project, 0)
    put(0, q, q_o)
    put(1, k, k_o)
    put(2, v, v_o)
    parts = halves()

    def row(r, _):
        span = pl.ds(pl.multiple_of(r * seqlen, seqlen), seqlen)
        same = seg_col[span] == seg_row[r]
        bias[...] = jnp.where(same, 0.0, masked_score).astype(F32)

        def pair(p, _):
            lanes = pl.ds(pl.multiple_of(p * 128, 128), 128)
            qp = q[span, lanes] * jnp.asarray(0.125, BF)
            kp = k[span, lanes]
            vp = v[span, lanes]
            total = None
            for half, part in enumerate(parts):
                s = dot(kp * part, qp, 1, 1) + bias[...]
                top = jnp.max(s, axis=0, keepdims=True)
                e = jnp.exp(s - top)
                mass = jnp.sum(e, axis=0, keepdims=True)
                prob = (e * (1.0 / mass)).astype(BF)
                c = dot(vp * part, prob, 0, 0)
                total = c if total is None else total + c
                lse_o[r * pairs * 2 + p * 2 + half] = top + jnp.log(mass)
            ctx[span, lanes] = total.T.astype(BF)
            return 0

        lax.fori_loop(0, pairs, pair, 0)
        return 0

    lax.fori_loop(0, nrow, row, 0)
    put(3, ctx, c_o)
    loads[3].wait()

    def attend(i, _):
        first = x_in[tile(i)].astype(F32) + dot(ctx[tile(i)], wo[...], 1, 0) + bo[...]
        z, rate = normalise(first)
        normed = z * g1[...] + s1[...]
        nf[tile(i)] = normed
        nb[tile(i)] = normed.astype(BF)
        z1[tile(i)] = z.astype(BF)
        r1[tile(i)] = jnp.broadcast_to(rate, (TM, 128))
        return 0

    lax.fori_loop(0, rows // TM, attend, 0)
    put(4, nb, nb_o)
    put(5, z1, z1_o)
    put(6, r1, r1_o)
    loads[4].wait()
    loads[5].wait()
    TF = 512

    def feed(i, _):
        def block(j, _):
            cols = pl.ds(pl.multiple_of(j * TF, TF), TF)
            h = dot(nb[tile(i)], wi[:, cols], 1, 0) + bi[:, cols]
            cdf = 0.5 + 0.5 * lax.erf(h * 0.7071067811865476)
            act_b = (h * cdf).astype(BF)
            act[tile(i), cols] = act_b
            slope = cdf + h * (0.3989422804014327 * jnp.exp(-0.5 * h * h))
            dg[tile(i), cols] = slope.astype(BF)
            return 0

        lax.fori_loop(0, inner // TF, block, 0)
        second = nf[tile(i)] + dot(act[tile(i)], w2[...], 1, 0) + b2[...]
        z, rate = normalise(second)
        final = z * g2[...] + s2[...]
        fin[tile(i)] = final
        lout[tile(i)] = final.astype(BF)
        z2[tile(i)] = z.astype(BF)
        r2[tile(i)] = jnp.broadcast_to(rate, (TM, 128))
        return 0

    lax.fori_loop(0, rows // TM, feed, 0)
    put(7, act, act_o)
    put(8, dg, dg_o)
    put(9, z2, z2_o)
    put(10, r2, r2_o)
    put(11, lout, out_o)
    for r in range(nrow):
        kinds = lax.broadcasted_iota(jnp.int32, (S_ROW, seqlen), 0)
        onehot = (seg_row[r] == kinds).astype(F32)
        count = jnp.sum(onehot, axis=1, keepdims=True)
        got = dot(onehot, fin[r * seqlen : (r + 1) * seqlen], 1, 0, HIGH)
        pool_o[r * S_ROW : (r + 1) * S_ROW] = got / count
    for c in stores:
        c.wait()


def forward(tokens, segment, wq, bq, wk, wv, bv, wo, bo, g1, s1, wi, bi, w2, b2, g2, s2):
    rows, width = tokens.shape
    nrow, seqlen = segment.shape
    inner = wi.shape[1]
    heads = width // 64
    vm = pl.BlockSpec(memory_space=pltpu.VMEM)
    hbm = pl.BlockSpec(memory_space=pl.ANY)
    act = (rows, width)
    wide = (rows, inner)
    sd = jax.ShapeDtypeStruct
    outs = (
        sd(act, BF), sd(act, BF), sd(act, BF), sd(act, BF), sd(act, BF), sd(act, BF),
        sd((rows, 128), F32), sd(wide, BF), sd(wide, BF), sd(act, BF), sd((rows, 128), F32),
        sd((nrow * heads, 1, seqlen), F32), sd(act, BF), sd((nrow * S_ROW, width), F32),
    )
    row = lambda a: a.reshape(1, -1)
    return pl.pallas_call(
        forward_kernel,
        name="forward",
        out_shape=outs,
        in_specs=[vm, vm, vm, hbm, vm, hbm, hbm, vm, hbm, vm, vm, vm, hbm, vm, hbm, vm, vm, vm],
        out_specs=[hbm] * 11 + [vm, hbm, vm],
        scratch_shapes=[pltpu.VMEM((width, width), BF)] * 4
        + [pltpu.VMEM((width, inner), BF), pltpu.VMEM((inner, width), BF)]
        + [pltpu.VMEM(act, BF)] * 4
        + [pltpu.VMEM(act, F32), pltpu.VMEM(act, BF), pltpu.VMEM(act, BF), pltpu.VMEM((rows, 128), F32)]
        + [pltpu.VMEM(wide, BF), pltpu.VMEM(wide, BF), pltpu.VMEM(act, BF), pltpu.VMEM((rows, 128), F32)]
        + [pltpu.VMEM(act, F32), pltpu.VMEM(act, BF), pltpu.VMEM((seqlen, seqlen), F32)]
        + [pltpu.SemaphoreType.DMA((6,)), pltpu.SemaphoreType.DMA((12,))],
        compiler_params=pltpu.CompilerParams(vmem_limit_bytes=64000000),
    )(
        tokens, segment.reshape(nrow, 1, seqlen), segment.reshape(rows, 1), wq, row(bq), wk, wv,
        row(bv), wo, row(bo), row(g1), row(s1), wi, row(bi), w2, row(b2), row(g2), row(s2),
    )


MESH = pl.DeviceIdType.MESH

def bit_dims(dp_size, bucket_size):
    dims = []
    for axis, size in ((1, bucket_size), (0, dp_size)):
        bit = 1
        while bit < size:
            dims.append((axis, bit))
            bit *= 2
    return dims

class Route:
    def __init__(self, dims):
        self.dims = dims
        self.pos = (lax.axis_index("dp"), lax.axis_index("bucket"))
        self.bits = [(self.pos[a] // b) % 2 for a, b in dims]

    def weights(self, stage, colour=0):
        core = self.bits[0]
        n = len(self.dims)
        if stage == 0 or n < 3:
            return {stage: 1}
        if n != 5 or isinstance(colour, int):
            if stage in (1, 2):
                return {stage: 1 - core, 3 - stage: core}
            return {stage: 1}
        keep = 1 - colour
        table = {
            1: {1: keep * (1 - core), 2: keep * core, 3: colour},
            2: {2: keep * (1 - core), 1: keep * core, 4: colour},
            3: {3: keep, 1: colour * (1 - core), 2: colour * core},
            4: {4: keep, 2: colour * (1 - core), 1: colour * core},
        }
        return table[stage]

    def bit(self, stage, colour=0):
        w = self.weights(stage, colour)
        return sum(v * self.bits[k] for k, v in w.items())

    def partner(self, stage, colour=0):
        where = list(self.pos)
        for k, v in self.weights(stage, colour).items():
            axis, bit = self.dims[k]
            where[axis] = where[axis] + v * (bit * (1 - 2 * self.bits[k]))
        return tuple(where)

def colour_of(c):
    return 1 - ((2 * c) % 9 + 7) // 9

def ar_kernel(dims, nblk, colours, *refs):
    ins = refs[:6]
    vec_in, out, vec_out, grads = refs[6:10]
    S = len(dims)
    stages = refs[10:10 + S]
    vbuf, vrecv, isem, ssem, rsem, osem, vs, vr, freed = refs[10 + S:]
    blk = grads.shape[1]
    rows = grads.shape[0]
    CH = 8 << S
    C = rows // CH
    width = grads.shape[1]
    route = Route(dims)
    bar = pltpu.get_barrier_semaphore()
    for k in range(S):
        axis, bit = dims[k]
        where = list(route.pos)
        where[axis] = where[axis] + bit * (1 - 2 * route.bits[k])
        pl.semaphore_signal(bar, inc=1, device_id=tuple(where), device_id_type=MESH)
    srcs = []
    for r in ins:
        h, w = r.shape
        for i in range(h // blk):
            for j in range(w // width):
                srcs.append(r.at[pl.ds(i * blk, blk), pl.ds(j * width, width)])
    for b, s in enumerate(srcs):
        pltpu.make_async_copy(s, grads.at[pl.ds(b * blk, blk)], isem.at[b]).start()
    vbuf[0] = vec_in[...]
    pl.semaphore_wait(bar, S)

    def col(c):
        return colour_of(c) if colours else 0
    def base(s, c):
        o = c * CH
        for k in range(s):
            o = o + route.bit(k, col(c)) * (CH >> (k + 1))
        return o
    def rs(s, c):
        half = CH >> (s + 1)
        b = route.bit(s, col(c))
        o = base(s, c)
        keep = pl.multiple_of(o + b * half, 8)
        send = pl.multiple_of(o + (1 - b) * half, 8)
        land = pl.multiple_of(c * half, 8)
        cp = pltpu.make_async_remote_copy(grads.at[pl.ds(send, half)], stages[s].at[pl.ds(land, half)],
            ssem.at[s, c], rsem.at[s, c], device_id=route.partner(s, col(c)), device_id_type=MESH)
        return cp, keep, land, half
    def ag(s, c):
        half = CH >> (s + 1)
        keep = pl.multiple_of(base(s, c) + route.bit(s, col(c)) * half, 8)
        return pltpu.make_async_remote_copy(grads.at[pl.ds(keep, half)], grads.at[pl.ds(keep, half)],
            ssem.at[2 * S - 1 - s, c], rsem.at[2 * S - 1 - s, c], device_id=route.partner(s, col(c)), device_id_type=MESH)
    def outc(c):
        o = pl.multiple_of(c * CH, 8)
        return pltpu.make_async_copy(grads.at[pl.ds(o, CH)], out.at[pl.ds(o, CH)], osem.at[c])
    def need(c):
        return ((c + 1) * CH + blk - 1) // blk
    def start(p, c):
        if p == 0:
            def w(b, _):
                pltpu.make_async_copy(srcs[0], grads.at[pl.ds(pl.multiple_of(b * blk, 8), blk)], isem.at[b]).wait()
                return 0
            lo = need(c - 1)
            lax.fori_loop(lo, need(c), w, 0)
        if p < S:
            rs(p, c)[0].start()
        elif p < 2 * S:
            pl.semaphore_wait(freed.at[2 * S - 1 - p, c], 1)
            ag(2 * S - 1 - p, c).start()
        else:
            outc(c).start()
    def finish(p, c):
        if p < S:
            cp, keep, land, half = rs(p, c)
            cp.wait_recv()
            grads[pl.ds(keep, half)] = grads[pl.ds(keep, half)] + stages[p][pl.ds(land, half)]
            cp.wait_send()
            pl.semaphore_signal(freed.at[p, c], inc=1, device_id=route.partner(p, col(c)), device_id_type=MESH)
        elif p < 2 * S:
            ag(2 * S - 1 - p, c).wait()
        else:
            outc(c).wait()
    def vcopy(r):
        axis, bit = dims[r]
        where = list(route.pos)
        where[axis] = where[axis] + bit * (1 - 2 * route.bits[r])
        return pltpu.make_async_remote_copy(vbuf.at[r], vrecv.at[r], vs.at[r], vr.at[r], device_id=tuple(where), device_id_type=MESH)
    NP = 2 * S + 1
    def step(t, _):
        for p in range(NP):
            c = t - 2 * p
            @pl.when((c >= 0) & (c < C))
            def _():
                start(p, c)
        for r in range(S):
            @pl.when(t == 2 + 2 * r)
            def _():
                vcopy(r).start()
        for p in range(NP):
            c = t - 1 - 2 * p
            @pl.when((c >= 0) & (c < C))
            def _():
                finish(p, c)
        for r in range(S):
            @pl.when(t == 3 + 2 * r)
            def _():
                cp = vcopy(r)
                cp.wait()
                vbuf[r + 1] = vbuf[r] + vrecv[r]
        return 0
    lax.fori_loop(0, C + 2 * (NP - 1) + 1, step, 0)
    vec_out[...] = vbuf[S]

def all_reduce(parts, vec, dp_size, bucket_size, colours=False):
    dims = bit_dims(dp_size, bucket_size)
    S = len(dims)
    width = parts[0].shape[1]
    rows = sum(p.size for p in parts) // width
    nblk = rows // width
    CH = 8 << S
    f32 = jnp.float32
    any_spec = pl.BlockSpec(memory_space=pl.ANY)
    vm = pl.BlockSpec(memory_space=pltpu.VMEM)
    return pl.pallas_call(
        functools.partial(ar_kernel, dims, nblk, colours),
        out_shape=(jax.ShapeDtypeStruct((rows, width), f32), jax.ShapeDtypeStruct(vec.shape, f32)),
        in_specs=[any_spec] * 6 + [vm], out_specs=(any_spec, vm),
        scratch_shapes=[pltpu.VMEM((rows, width), f32)]
        + [pltpu.VMEM((rows >> (s + 1), width), f32) for s in range(S)]
        + [pltpu.VMEM((S + 1,) + vec.shape, f32), pltpu.VMEM((S,) + vec.shape, f32),
           pltpu.SemaphoreType.DMA((nblk,)), pltpu.SemaphoreType.DMA((2 * S, rows // CH)), pltpu.SemaphoreType.DMA((2 * S, rows // CH)),
           pltpu.SemaphoreType.DMA((rows // CH,)), pltpu.SemaphoreType.DMA((S,)), pltpu.SemaphoreType.DMA((S,)),
           pltpu.SemaphoreType.REGULAR((S, rows // CH))],
        compiler_params=pltpu.CompilerParams(collective_id=1, has_side_effects=True, vmem_limit_bytes=67043328),
    )(*parts, vec)


cos_scale = 20.0


def gather_order(dims, dp_size, bucket_size, own):
    S = len(dims)
    n = np.arange(dp_size * bucket_size)
    key = [(n >> (S - 1 - s)) & 1 for s in range(S)]
    if S >= 3:
        core = key[0]
        key[1], key[2] = np.where(core == 1, key[2], key[1]), np.where(core == 1, key[1], key[2])
    pos = [0, 0]
    for (axis, bit), value in zip(dims, key):
        pos[axis] = pos[axis] + bit * value
    device = pos[0] * bucket_size + pos[1]
    return (device[:, None] * own + np.arange(own)[None, :]).reshape(1, -1).astype(np.int32)


def sphere(vectors):
    factor = lax.rsqrt(jnp.sum(vectors * vectors, axis=1, keepdims=True) + 1e-06)
    return vectors * factor, factor


def loss_kernel(dims, bucket_size, pool, sid, pair_row, pair_col, dpool, loss, buf, unit, weigh, ssem, rsem):
    own, width = pool.shape
    sents = buf.shape[0]
    pairs = sents // 2
    S = len(dims)
    route = Route(dims)
    bar = pltpu.get_barrier_semaphore()
    for k in range(S):
        axis, bit = dims[k]
        where = list(route.pos)
        where[axis] = where[axis] + bit * (1 - 2 * route.bits[k])
        pl.semaphore_signal(bar, inc=1, device_id=tuple(where), device_id_type=MESH)
    base = [0]
    for s in range(S):
        base.append(base[s] + route.bit(s) * (sents >> (s + 1)))
    buf[pl.ds(pl.multiple_of(base[S], 8), own)] = pool[...]
    pl.semaphore_wait(bar, S)
    for s in reversed(range(S)):
        half = sents >> (s + 1)
        here = pl.ds(pl.multiple_of(base[s + 1], 8), half)
        c = pltpu.make_async_remote_copy(
            buf.at[here], buf.at[here], ssem.at[s], rsem.at[s],
            device_id=route.partner(s), device_id_type=MESH,
        )
        c.start()
        c.wait()
    B = min(256, pairs)
    for i in range(sents // B):
        part = pl.ds(i * B, B)
        pick = (pair_col[part] == sid[...]).astype(F32)
        ordered = dot(pick, buf[...], 1, 0, HIGH)
        unit[part] = sphere(ordered)[0]
    total = jnp.zeros((1, 1), F32)
    for i in range(pairs // B):
        part = pl.ds(i * B, B)
        logits = cos_scale * dot(unit[part], unit[pairs:], 1, 1, HIGH)
        top = jnp.max(logits, axis=1, keepdims=True)
        row_lse = top + jnp.log(jnp.sum(jnp.exp(logits - top), axis=1, keepdims=True))
        line = lax.broadcasted_iota(jnp.int32, logits.shape, 0) + i * B
        eye = (line == lax.broadcasted_iota(jnp.int32, logits.shape, 1)).astype(F32)
        weigh[part] = jnp.exp(logits - row_lse) - eye
        gap = row_lse - jnp.sum(logits * eye, axis=1, keepdims=True)
        total = total + jnp.sum(gap, axis=0, keepdims=True)
    loss[...] = total
    first = (route.pos[0] * bucket_size + route.pos[1]) * own
    mine = lax.broadcasted_iota(jnp.int32, (own, sents), 0) + first
    choose = (mine == pair_row[...]).astype(F32)
    by_row = dot(choose[:, :pairs], weigh[...], 1, 0, HIGH)
    by_column = dot(choose[:, pairs:], weigh[...], 1, 1, HIGH)
    grad = cos_scale * (dot(by_row, unit[pairs:], 1, 0, HIGH) + dot(by_column, unit[:pairs], 1, 0, HIGH))
    u, factor = sphere(pool[...])
    dpool[...] = factor * (grad - u * jnp.sum(u * grad, axis=1, keepdims=True))


def pair_loss(pool, pair_order, dp_size, bucket_size):
    dims = bit_dims(dp_size, bucket_size)
    S = len(dims)
    own, width = pool.shape
    sents = pair_order.shape[0]
    vm = pl.BlockSpec(memory_space=pltpu.VMEM)
    sid = jnp.asarray(gather_order(dims, dp_size, bucket_size, own))
    return pl.pallas_call(
        functools.partial(loss_kernel, dims, bucket_size),
        name="pair_loss",
        out_shape=(jax.ShapeDtypeStruct(pool.shape, F32), jax.ShapeDtypeStruct((1, 1), F32)),
        in_specs=[vm] * 4, out_specs=(vm, vm),
        scratch_shapes=[
            pltpu.VMEM((sents, width), F32), pltpu.VMEM((sents, width), F32),
            pltpu.VMEM((sents // 2, sents // 2), F32),
            pltpu.SemaphoreType.DMA((S,)), pltpu.SemaphoreType.DMA((S,)),
        ],
        compiler_params=pltpu.CompilerParams(collective_id=2, has_side_effects=True, vmem_limit_bytes=60000000),
    )(pool, sid, pair_order.reshape(1, -1), pair_order.reshape(-1, 1))


def norm_grad(dx, z, rate, gain):
    dz = dx * gain
    mean = jnp.mean(dz, axis=-1, keepdims=True)
    cross = jnp.mean(dz * z, axis=-1, keepdims=True)
    return rate * (dz - mean - z * cross), jnp.sum(dx * z, axis=0), jnp.sum(dx, axis=0)


def local(
    dp_size, bucket_size,
    tokens, segment, pair_order, cotangent, query_weight, query_bias, key_weight, value_weight,
    value_bias, out_weight, out_bias, norm_gain, norm_shift, inner_weight, inner_bias,
    outer_weight, outer_bias, final_gain, final_shift,
):
    nrows, seqlen = segment.shape
    width = tokens.shape[1]
    (
        query_b, key_b, value_b, context_b, normed_b, z1, r1, active_b, slope, z2, r2, lse,
        layer_out, pooled,
    ) = forward(
        tokens, segment, query_weight, query_bias, key_weight, value_weight, value_bias,
        out_weight, out_bias, norm_gain, norm_shift, inner_weight, inner_bias, outer_weight,
        outer_bias, final_gain, final_shift,
    )
    dpooled, loss_value = pair_loss(pooled, pair_order, dp_size, bucket_size)
    loss_value = loss_value.reshape(())
    onehot = (segment[:, None, :] == jnp.arange(S_ROW, dtype=jnp.int32)[None, :, None]).astype(F32)
    counts = jnp.sum(onehot, axis=2, keepdims=True)
    spread = jnp.einsum(
        "rsl,rsd->rld", onehot, dpooled.reshape(nrows, S_ROW, width) / counts, precision=HIGH
    )
    grad_final = cotangent.astype(F32) + spread.reshape(nrows * seqlen, width)
    grad_second, dfinal_gain, dfinal_shift = norm_grad(
        grad_final, z2.astype(F32), r2[:, :1], final_gain
    )
    grad_second_b = grad_second.astype(BF)
    douter_weight = dot(active_b, grad_second_b, 0, 0)
    douter_bias = jnp.sum(grad_second, axis=0)
    grad_inner = dot(grad_second_b, outer_weight, 1, 1) * slope.astype(F32)
    grad_inner_b = grad_inner.astype(BF)
    dinner_weight = dot(normed_b, grad_inner_b, 0, 0)
    dinner_bias = jnp.sum(grad_inner, axis=0)
    grad_normed = grad_second + dot(grad_inner_b, inner_weight, 1, 1)
    grad_first, dnorm_gain, dnorm_shift = norm_grad(
        grad_normed, z1.astype(F32), r1[:, :1], norm_gain
    )
    grad_first_b = grad_first.astype(BF)
    dout_weight = dot(context_b, grad_first_b, 0, 0)
    dout_bias = jnp.sum(grad_first, axis=0)
    split = lambda a: a.reshape(nrows, seqlen, H, HD)
    grad_context = split(dot(grad_first_b, out_weight, 1, 1).astype(BF))
    query_h, key_h, value_h = split(query_b), split(key_b), split(value_b)
    same = segment[:, None, :, None] == segment[:, None, None, :]
    ein = functools.partial(jnp.einsum, preferred_element_type=F32)
    scores = jnp.where(same, ein("rqhe,rkhe->rhqk", query_h, key_h) * 0.125, masked_score)
    probs = jnp.exp(scores - lse.reshape(nrows, H, seqlen, 1))
    probs_b = probs.astype(BF)
    grad_probs = ein("rqhe,rkhe->rhqk", grad_context, value_h)
    grad_value = ein("rhqk,rqhe->rkhe", probs_b, grad_context)
    grad_scores = probs * (grad_probs - jnp.sum(probs * grad_probs, axis=-1, keepdims=True))
    grad_scores_b = grad_scores.astype(BF)
    grad_query = ein("rhqk,rkhe->rqhe", grad_scores_b, key_h) * 0.125
    grad_key = ein("rhqk,rqhe->rkhe", grad_scores_b, query_h) * 0.125
    grad_query = grad_query.reshape(nrows * seqlen, width)
    grad_key = grad_key.reshape(nrows * seqlen, width)
    grad_value = grad_value.reshape(nrows * seqlen, width)
    dquery_bias = jnp.sum(grad_query, axis=0)
    dvalue_bias = jnp.sum(grad_value, axis=0)
    grad_query_b = grad_query.astype(BF)
    grad_key_b = grad_key.astype(BF)
    grad_value_b = grad_value.astype(BF)
    dquery_weight = dot(tokens, grad_query_b, 0, 0)
    dkey_weight = dot(tokens, grad_key_b, 0, 0)
    dvalue_weight = dot(tokens, grad_value_b, 0, 0)
    tokens_grad = (
        grad_first
        + dot(grad_query_b, query_weight, 1, 1)
        + dot(grad_key_b, key_weight, 1, 1)
        + dot(grad_value_b, value_weight, 1, 1)
    )
    vectors = [
        dquery_bias, dvalue_bias, dout_bias, dnorm_gain, dnorm_shift,
        dinner_bias, douter_bias, dfinal_gain, dfinal_shift,
    ]
    packed = jnp.concatenate(vectors).reshape(-1, width)
    nvec = packed.shape[0]
    packed = jnp.pad(packed, ((0, -nvec % 8), (0, 0)))
    flat, packed = all_reduce(
        [douter_weight, dinner_weight, dout_weight, dquery_weight, dkey_weight, dvalue_weight],
        packed, dp_size, bucket_size, True,
    )
    blocks = flat.reshape(-1, width, width)
    wide = inner_weight.shape[1] // width
    douter_weight = flat[: wide * width]
    dinner_weight = jnp.concatenate([blocks[wide + j] for j in range(wide)], axis=1)
    dout_weight, dquery_weight, dkey_weight, dvalue_weight = (blocks[2 * wide + j] for j in range(4))
    packed = packed[:nvec].reshape(-1)
    sizes = [v.shape[0] for v in vectors]
    ends = [sum(sizes[: i + 1]) for i in range(len(sizes))]
    (
        dquery_bias, dvalue_bias, dout_bias, dnorm_gain, dnorm_shift,
        dinner_bias, douter_bias, dfinal_gain, dfinal_shift,
    ) = (packed[e - n : e] for e, n in zip(ends, sizes))
    return (
        layer_out, loss_value, tokens_grad, dquery_weight, dquery_bias, dkey_weight,
        dvalue_weight, dvalue_bias, dout_weight, dout_bias, dnorm_gain, dnorm_shift,
        dinner_weight, dinner_bias, douter_weight, douter_bias, dfinal_gain, dfinal_shift,
    )


def solution(mesh):
    split = P(("dp", "bucket"), None)
    return jax.shard_map(
        functools.partial(local, mesh.shape["dp"], mesh.shape["bucket"]),
        mesh=mesh,
        in_specs=(split, split, P(), split) + (P(),) * 15,
        out_specs=(split, P(), split) + (P(),) * 15,
        check_vma=False,
    )
```

time: 659 us -> 580 us (0.88)
  matrix products: 212 us -> 130 us
  Pallas kernels: 249 us -> 330 us
  waiting for transfers between devices: 57.5 us -> 0 us
  other arithmetic: 54.5 us -> 33.8 us
  between operations: 15.1 us -> 3.25 us
  local copies, waits for them, and re-layouts: 61.9 us -> 72.4 us
    pallas_call x0 -> x2, Pallas kernels: none -> 84.2 us  [the longest x1 49.9 us: forward(): pl.pallas_call(forward_kernel, name='forward', out_shape=outs, in_specs=[...]
    dot_general x30 -> x17, matrix products: 210 us -> 128 us  [the longest x12 68.2 us: dot(): lax.dot_general(a, b, (((da,), (db,)), ((), ())), precision=precision, pr...]
    all_gather x1 -> x0, waiting for transfers between devices: 57.5 us -> none  [local(): pooled_every = lax.all_gather(pooled, ('dp', 'bucket'), axis=0, tiled=True)]
    reduce_sum x9 -> x1, other arithmetic: 21.6 us -> 1.41 us  [norm_grad(): jnp.sum(dx * z, axis=0)]
    reshape x4 -> x14, local copies, waits for them, and re-layouts: 10.3 us -> 24.9 us  [the longest x4 12 us: local(): split = lambda a: a.reshape(nrows, seqlen, H, HD)]
    pallas_call x0 -> x3, local copies, waits for them, and re-layouts: none -> 6.89 us  [forward(): pl.pallas_call(forward_kernel, name='forward', out_shape=outs, in_specs=[...]
    convert_element_type x2 -> x1, other arithmetic: 23.2 us -> 21.5 us  [local(): grad_scores_b = grad_scores.astype(BF)]
  transfers between devices with their start and end apart: 1 -> 0, of which waited for: 1 -> 0; matrix products, arithmetic and copies ran while one was open for 0% -> 0% of each run, Pallas kernels for 0% -> 0%
where the time goes in v2:
time: 580 us; the launch traced here: 569 us
  Pallas kernels  330 us (57%)
  matrix products  130 us (22%)
  local copies, waits for them, and re-layouts  72.4 us (12%)
  other arithmetic  33.8 us (6%)
    pallas_call x1, Pallas kernels, all_reduce(): pl.pallas_call(functools.partial(ar_kernel, dims, nblk, colours), out_sha...  246 us
    dot_general x12, matrix products, dot(): lax.dot_general(a, b, (((da,), (db,)), ((), ())), precision=precision, pr...  68.2 us
    pallas_call x1, Pallas kernels, forward(): pl.pallas_call(forward_kernel, name='forward', out_shape=outs, in_specs=[...  49.9 us
    pallas_call x1, Pallas kernels, pair_loss(): pl.pallas_call(functools.partial(loss_kernel, dims, bucket_size), name='p...  34.3 us
    convert_element_type x1, other arithmetic, local(): grad_scores_b = grad_scores.astype(BF)  21.5 us
    dot_general x1, matrix products, local(): grad_probs = ein('rqhe,rkhe->rhqk', grad_context, value_h)  21 us
    dot_general x1, matrix products, local(): grad_value = ein('rhqk,rqhe->rkhe', probs_b, grad_context)  13.9 us
    reshape x4, local copies, waits for them, and re-layouts, local(): split = lambda a: a.reshape(nrows, seqlen, H, HD)  12 us

profile of v2, /device:TPU:0, one launch (start us, length us, event | category | flops | bytes accessed | tf_op | source)
XLA Modules:
  0.0 569.4 jit_solution(6228329312630299550)
XLA Ops:
  1.4 1.3 reshape.167.bq
  2.7 1.3 reshape.168.bv
  4.0 1.3 reshape.169.bo
  12.3 1.3 reshape.165.seg_row
  13.5 1.6 copy.52.pair_col
  16.1 1.9 broadcast_compare_fusion
  18.1 49.9 %forward.1 = (bf16[1024,768]{1,0:T(8,128)(2,1)}, bf16[1024,768]{1,0:T(8,128)(2,1)}, bf16[1024,768]{1,0:T(8,128)(2,1)}, bf16[1024,768]{1,0:T(8,128)(2,1)}, bf16[1...) custom-call(bf16[1024,768]{1,0:T(8,128)(2,1)} %x_in.1, ...), custom_call_target="tpu_custom_call" | custom-call | tf_op jit(solution)/shard_map/forward/pallas_call | solution.py:186
  68.0 34.3 %pair_loss.1 = (f32[16,768]{1,0:T(8,128)}, f32[1,1]{1,0:T(1,128)}) custom-call(f32[16,768]{1,0:T(8,128)} %get-tuple-element.37.pool, s32[1,512]{1,0:T(1,128)} %constant.17.clone.sid, s32[1,512]{1,0:T(1,128)} %bitcast.99, s32[512,1]{1,0:T(8,128)} %copy.52.pair_col), custom_call_target="tpu_custom_call" | custom-call | tf_op jit(solution)/shard_map/pair_loss/pallas_call | solution.py:474
  102.3 1.5 slice_reduce_fusion
  104.8 1.7 copy.53
  106.5 1.4 reshape.181
  107.9 2.6 copy.54
  110.5 2.9 reshape.182
  113.4 2.6 copy.58
  116.0 3.9 reshape.184
  119.9 1.5 fusion.32
  121.7 1.4 fusion.9
  123.2 1.5 fusion.41
  124.7 7.7 %fusion.28.refs_0_ = f32[3072,768]{1,0:T(8,128)} fusion(bf16[1024,3072]{1,0:T(8,128)(2,1)S(1)} %bitcast.101, f32[1024,768]{1,0:T(8,128)S(1)} %get-tuple-element.71), kind=kOutput, calls=%fused_computation.53 | convolution fusion | flops 4832624640 | bytes 18874368 | tf_op jit(solution)/shard_map/dot_general | solution.py:22
  132.5 9.9 %fusion.4 = (f32[3072]{0:T(1024)S(1)}, f32[1024,3072]{1,0:T(8,128)}) fusion(bf16[1024,3072]{1,0:T(8,128)(2,1)} %get-tuple-element.43, bf16[3072,768]{1,0:T(8,128)(2,1)S(1)} %bitcast.87, f32[1024,768]{1,0:T(8,128)S(1)} %get-tuple-element.71), kind=kOutput, calls=%fused_computation.8 | convolution fusion | flops 4842058752 | bytes 26750976 | tf_op jit(solution)/shard_map/dot_general | solution.py:22
  142.4 11.3 %fusion.13 = (f32[768]{0:T(1024)S(1)}, f32[1024]{0:T(1024)S(1)}, f32[1024]{0:T(1024)S(1)}, f32[768]{0:T(1024)S(1)}, f32[1024,768]{1,0:T(8,128)S(1)}) fusion(bf16[1024,768]{1,0:T(8,128)(2,1)} %get-tuple-element.44, f32[768]{0:T(1024)S(1)} %copy-done.20, f32[1024,768]{1,0:T(8,128)} %copy-done.9, bf16[768,3072]{1,0:T(8,128)(2,1)S(1)} %bitcast.89, ...), kind=kOutput, calls=%fused_computation.23 | convolution fusion | flops 4848349184 | bytes 31474688 | tf_op jit(solution)/shard_map/dot_general | solution.py:22
  153.8 11.8 %fusion.38.refs_1_ = f32[768,3072]{1,0:T(8,128)} fusion(bf16[1024,768]{1,0:T(8,128)(2,1)} %get-tuple-element.50, f32[1024,3072]{1,0:T(8,128)} %get-tuple-element.90, bf16[1024,3072]{1,0:T(8,128)(2,1)} %get-tuple-element.43), kind=kOutput, calls=%fused_computation.89 | convolution fusion | flops 4841275392 | bytes 29884416 | tf_op jit(solution)/shard_map/dot_general | solution.py:22
  167.0 2.9 fusion.25.refs_2_
  169.9 2.6 convolution_convert_fusion
  172.5 2.6 copy.57
  175.1 3.8 reshape.183
  179.0 10.1 %fusion.17 = f32[2,12,512,512]{2,3,1,0:T(8,128)} fusion(bf16[2,512,12,64]{1,0,3,2:T(2,128)(2,1)S(1)} %reshape.181, bf16[2,512,12,64]{1,0,3,2:T(2,128)(2,1)S(1)} %reshape.182), kind=kOutput, calls=%fused_computation.41 | convolution fusion | flops 805306368 | bytes 28311552 | tf_op jit(solution)/shard_map/rqhe,rkhe->rhqk/dot_general | solution.py:541
  189.0 13.9 %bitcast_convert_fusion = (bf16[2,512,12,64]{1,3,2,0:T(8,128)(2,1)}, f32[2,12,64,512]{3,2,1,0:T(8,128)}) fusion(f32[2,12,512,512]{2,3,1,0:T(8,128)} %fusion.17, f32[2,12,512]{2,1,0:T(8,128)S(1)} %sub.46, pred[2,512,512]{1,2,0:T(8,128)(4,1)S(1)} %copy-done.6, bf16[2,512,12,64]{1,0,3,2:T(2,128)(2,1)S(1)} %copy-done.2), kind=kOutput, calls=%fused_computation.25 | convolution fusion | flops 831258624 | bytes 32030720 | tf_op jit(solution)/shard_map/rhqk,rqhe->rkhe/dot_general | solution.py:545
  202.9 3.2 copy.69
  206.1 1.6 copy.84
  208.0 4.7 convolution_bitcast_fusion.refs_5_
  212.7 21.0 %multiply_reduce_fusion = (f32[2,12,512]{2,1,0:T(8,128)S(1)}, f32[2,12,512,512]{2,3,1,0:T(8,128)}) fusion(f32[2,12,512,512]{2,3,1,0:T(8,128)} %fusion.17, f32[2,12,512]{2,1,0:T(8,128)S(1)} %sub.46, pred[2,512,512]{1,2,0:T(8,128)(4,1)} %broadcast_compare_fusion, bf16[2,512,12,64]{1,0,3,2:T(2,128)(2,1)} %reshape.184, bf16[2,512,12,64]{1,0,3,2:T(2,128)(2,1)} %reshape.183), kind=kOutput, calls=%fused_computation.1 | convolution fusion | flops 836751360 | bytes 54099968 | tf_op jit(solution)/shard_map/rqhe,rkhe->rhqk/dot_general | solution.py:544
  233.7 21.5 %multiply_convert_fusion = bf16[2,12,512,512]{2,3,1,0:T(8,128)(2,1)} fusion(f32[2,12,512,512]{2,3,1,0:T(8,128)} %get-tuple-element.84, f32[2,12,512,512]{2,3,1,0:T(8,128)} %fusion.17, f32[2,12,512]{2,1,0:T(8,128)S(1)} %get-tuple-element.83, f32[2,12,512]{2,1,0:T(8,128)S(1)} %sub.46, pred[2,512,512]{1,2,0:T(8,128)(4,1)} %broadcast_compare_fusion), kind=kLoop, calls=%fused_computation | loop fusion | flops 37748736 | bytes 63537152 | tf_op jit(solution)/shard_map/convert_element_type | solution.py:547
  255.2 8.5 %fusion.16 = bf16[2,512,12,64]{1,3,2,0:T(8,128)(2,1)S(1)} fusion(bf16[2,12,512,512]{2,3,1,0:T(8,128)(2,1)} %multiply_convert_fusion, bf16[2,512,12,64]{1,0,3,2:T(2,128)(2,1)S(1)} %reshape.182), kind=kOutput, calls=%fused_computation.40 | convolution fusion | flops 806879232 | bytes 15728640 | tf_op jit(solution)/shard_map/rhqk,rqhe->rkhe/dot_general | solution.py:549
  263.7 6.6 %bitcast_convert_fusion.1 = (bf16[2,512,12,64]{1,3,2,0:T(8,128)(2,1)S(1)}, f32[2,12,64,512]{3,2,1,0:T(8,128)S(1)}) fusion(bf16[2,12,512,512]{2,3,1,0:T(8,128)(2,1)} %multiply_convert_fusion, bf16[2,512,12,64]{1,0,3,2:T(2,128)(2,1)S(1)} %reshape.181), kind=kOutput, calls=%fused_computation.27 | convolution fusion | flops 806879232 | bytes 18874368 | tf_op jit(solution)/shard_map/rhqk,rkhe->rqhe/dot_general | solution.py:548
  270.3 1.6 copy.63
  272.4 1.6 copy.66
  274.0 1.6 copy.83
  276.7 4.4 convolution_bitcast_fusion.1.refs_4_
  281.1 3.1 fusion.47
  284.2 3.1 convolution_bitcast_fusion.2.refs_3_
  287.3 246.0 %shard_map.331 = (f32[9216,768]{1,0:T(8,128)}, f32[16,768]{1,0:T(8,128)}) custom-call(f32[3072,768]{1,0:T(8,128)} %fusion.28.refs_0_, f32[768,3072]{1,0:T(8,128)} %fusion.38.refs_1_, f32[768,768]{1,0:T(8,128)} %fusion.25.refs_2_, f32[768,768]{1,0:T(8,128)} %convolution_bitcast_fusion.2.refs_3_, f32[768,768]{1,0:T(8,128)} %convolution_bitcast_fusion.1.refs_4_, ...), custom_call_target="tpu_custom_call" | custom-call | tf_op jit(solution)/shard_map/pallas_call | solution.py:377
  534.1 1.7 slice_reduce_fusion.2
  536.5 3.3 fusion.46
  540.9 3.2 add_add_fusion
  544.1 8.0 %slice.127 = f32[3072,768]{1,0:T(8,128)} slice(f32[9216,768]{1,0:T(8,128)} %get-tuple-element.52), slice={[0:3072], [0:768]} | slice | bytes 18874368 | tf_op jit(solution)/shard_map/slice | solution.py:580
  552.1 10.9 %fusion.45 = (f32[768,768]{1,0:T(8,128)S(1)}, f32[768,768]{1,0:T(8,128)S(1)}, f32[768,768]{1,0:T(8,128)S(1)}, f32[768,768]{1,0:T(8,128)S(1)}, f32[768,768]{1,0:T...) fusion(f32[9216,768]{1,0:T(8,128)} %get-tuple-element.52), kind=kLoop, calls=%fused_computation.92 | loop fusion | bytes 37748736 | tf_op jit(solution)/shard_map/slice | solution.py:581
  563.1 4.2 pad_maximum_fusion
  (92 shorter events, 15.9 us)
Async XLA Ops:
  113.4 6.5 %copy-start.17 = (s32[2,512]{1,0:T(2,128)S(1)}, s32[2,512]{1,0:T(2,128)}, u32[]{:S(2)}) copy-start(s32[2,512]{1,0:T(2,128)} %param.21) | copy-start | bytes 12292
  113.4 6.5 %copy-start.18 = (f32[16,768]{1,0:T(8,128)S(1)}, f32[16,768]{1,0:T(8,128)}, u32[]{:S(2)}) copy-start(f32[16,768]{1,0:T(8,128)} %get-tuple-element.41) | copy-start | bytes 147460
  116.0 5.4 copy-start.19
  119.9 1.5 copy-start.4
  119.9 1.9 copy-start.5
  119.9 4.8 slice-start.4
  121.7 2.9 slice-start.5
  123.2 9.3 %slice-start = ((s8[4718592]{0:T(1024)(128)(4,1)}), s8[4194304]{0:T(1024)(128)(4,1)S(1)}, s32[]{:S(2)}) async-start(s8[4718592]{0:T(1024)(128)(4,1)} %bitcast.86), calls=%async_computation | async-start | bytes 8388608
  123.2 19.2 %slice-start.2 = ((s8[4718592]{0:T(1024)(128)(4,1)}), s8[4194304]{0:T(1024)(128)(4,1)S(1)}, s32[]{:S(2)}) async-start(s8[4718592]{0:T(1024)(128)(4,1)} %bitcast.88), calls=%async_computation.2 | async-start | bytes 8388608
  124.7 7.8 %copy-start.9 = (f32[1024,768]{1,0:T(8,128)}, f32[1024,768]{1,0:T(8,128)S(1)}, u32[]{:S(2)}) copy-start(f32[1024,768]{1,0:T(8,128)S(1)} %get-tuple-element.71) | copy-start | bytes 9437188
  124.7 7.8 %slice-start.1 = ((s8[4718592]{0:T(1024)(128)(4,1)}), s8[524288]{0:T(1024)(128)(4,1)S(1)}, s32[]{:S(2)}) async-start(s8[4718592]{0:T(1024)(128)(4,1)} %bitcast.86), calls=%async_computation.1 | async-start | bytes 1048576
  124.7 17.7 %slice-start.3 = ((s8[4718592]{0:T(1024)(128)(4,1)}), s8[524288]{0:T(1024)(128)(4,1)S(1)}, s32[]{:S(2)}) async-start(s8[4718592]{0:T(1024)(128)(4,1)} %bitcast.88), calls=%async_computation.3 | async-start | bytes 1048576
  132.5 9.9 %copy-start.20 = (f32[768]{0:T(1024)S(1)}, f32[768]{0:T(1024)}, u32[]{:S(2)}) copy-start(f32[768]{0:T(1024)} %param.31) | copy-start | bytes 9220
  153.8 11.8 %copy-start.12 = (bf16[1024,768]{1,0:T(8,128)(2,1)S(1)}, bf16[1024,768]{1,0:T(8,128)(2,1)}, u32[]{:S(2)}) copy-start(bf16[1024,768]{1,0:T(8,128)(2,1)} %get-tuple-element.44) | copy-start | bytes 4718596
  165.6 1.4 copy-start.21
  166.7 3.2 copy-start
  167.0 2.9 copy-start.15
  178.9 10.1 %copy-start.2 = (bf16[2,512,12,64]{1,0,3,2:T(2,128)(2,1)S(1)}, bf16[2,512,12,64]{1,0,3,2:T(2,128)(2,1)}, u32[]{:S(2)}) copy-start(bf16[2,512,12,64]{1,0,3,2:T(2,128)(2,1)} %reshape.183) | copy-start | bytes 4718596
  179.0 10.1 %copy-start.6 = (pred[2,512,512]{1,2,0:T(8,128)(4,1)S(1)}, pred[2,512,512]{1,2,0:T(8,128)(4,1)}, u32[]{:S(2)}) copy-start(pred[2,512,512]{1,2,0:T(8,128)(4,1)} %broadcast_compare_fusion) | copy-start | bytes 1572868
  202.9 4.8 copy-start.8
  272.4 11.9 %copy-start.13 = (bf16[96,8,2,512]{3,1,2,0:T(8,128)(2,1)}, bf16[96,8,2,512]{3,1,2,0:T(8,128)(2,1)S(1)}, u32[]{:S(2)}) copy-start(bf16[96,8,2,512]{3,1,2,0:T(8,128)(2,1)S(1)} %copy.82) | copy-start | bytes 4718596
  274.0 2.7 copy-start.11
  276.7 4.4 copy-start.14
  276.7 4.4 copy-start.16
  536.4 3.4 copy-start.1
  536.4 3.4 copy-start.3
  536.4 3.5 copy-start.7
  536.4 4.5 copy-start.10

commit v3 on v2

--- a/solution.py
+++ b/solution.py
@@ -251,141 +251,6 @@
 
 def colour_of(c):
     return 1 - ((2 * c) % 9 + 7) // 9
-
-def ar_kernel(dims, nblk, colours, *refs):
-    ins = refs[:6]
-    vec_in, out, vec_out, grads = refs[6:10]
-    S = len(dims)
-    stages = refs[10:10 + S]
-    vbuf, vrecv, isem, ssem, rsem, osem, vs, vr, freed = refs[10 + S:]
-    blk = grads.shape[1]
-    rows = grads.shape[0]
-    CH = 8 << S
-    C = rows // CH
-    width = grads.shape[1]
-    route = Route(dims)
-    bar = pltpu.get_barrier_semaphore()
-    for k in range(S):
-        axis, bit = dims[k]
-        where = list(route.pos)
-        where[axis] = where[axis] + bit * (1 - 2 * route.bits[k])
-        pl.semaphore_signal(bar, inc=1, device_id=tuple(where), device_id_type=MESH)
-    srcs = []
-    for r in ins:
-        h, w = r.shape
-        for i in range(h // blk):
-            for j in range(w // width):
-                srcs.append(r.at[pl.ds(i * blk, blk), pl.ds(j * width, width)])
-    for b, s in enumerate(srcs):
-        pltpu.make_async_copy(s, grads.at[pl.ds(b * blk, blk)], isem.at[b]).start()
-    vbuf[0] = vec_in[...]
-    pl.semaphore_wait(bar, S)
-
-    def col(c):
-        return colour_of(c) if colours else 0
-    def base(s, c):
-        o = c * CH
-        for k in range(s):
-            o = o + route.bit(k, col(c)) * (CH >> (k + 1))
-        return o
-    def rs(s, c):
-        half = CH >> (s + 1)
-        b = route.bit(s, col(c))
-        o = base(s, c)
-        keep = pl.multiple_of(o + b * half, 8)
-        send = pl.multiple_of(o + (1 - b) * half, 8)
-        land = pl.multiple_of(c * half, 8)
-        cp = pltpu.make_async_remote_copy(grads.at[pl.ds(send, half)], stages[s].at[pl.ds(land, half)],
-            ssem.at[s, c], rsem.at[s, c], device_id=route.partner(s, col(c)), device_id_type=MESH)
-        return cp, keep, land, half
-    def ag(s, c):
-        half = CH >> (s + 1)
-        keep = pl.multiple_of(base(s, c) + route.bit(s, col(c)) * half, 8)
-        return pltpu.make_async_remote_copy(grads.at[pl.ds(keep, half)], grads.at[pl.ds(keep, half)],
-            ssem.at[2 * S - 1 - s, c], rsem.at[2 * S - 1 - s, c], device_id=route.partner(s, col(c)), device_id_type=MESH)
-    def outc(c):
-        o = pl.multiple_of(c * CH, 8)
-        return pltpu.make_async_copy(grads.at[pl.ds(o, CH)], out.at[pl.ds(o, CH)], osem.at[c])
-    def need(c):
-        return ((c + 1) * CH + blk - 1) // blk
-    def start(p, c):
-        if p == 0:
-            def w(b, _):
-                pltpu.make_async_copy(srcs[0], grads.at[pl.ds(pl.multiple_of(b * blk, 8), blk)], isem.at[b]).wait()
-                return 0
-            lo = need(c - 1)
-            lax.fori_loop(lo, need(c), w, 0)
-        if p < S:
-            rs(p, c)[0].start()
-        elif p < 2 * S:
-            pl.semaphore_wait(freed.at[2 * S - 1 - p, c], 1)
-            ag(2 * S - 1 - p, c).start()
-        else:
-            outc(c).start()
-    def finish(p, c):
-        if p < S:
-            cp, keep, land, half = rs(p, c)
-            cp.wait_recv()
-            grads[pl.ds(keep, half)] = grads[pl.ds(keep, half)] + stages[p][pl.ds(land, half)]
-            cp.wait_send()
-            pl.semaphore_signal(freed.at[p, c], inc=1, device_id=route.partner(p, col(c)), device_id_type=MESH)
-        elif p < 2 * S:
-            ag(2 * S - 1 - p, c).wait()
-        else:
-            outc(c).wait()
-    def vcopy(r):
-        axis, bit = dims[r]
-        where = list(route.pos)
-        where[axis] = where[axis] + bit * (1 - 2 * route.bits[r])
-        return pltpu.make_async_remote_copy(vbuf.at[r], vrecv.at[r], vs.at[r], vr.at[r], device_id=tuple(where), device_id_type=MESH)
-    NP = 2 * S + 1
-    def step(t, _):
-        for p in range(NP):
-            c = t - 2 * p
-            @pl.when((c >= 0) & (c < C))
-            def _():
-                start(p, c)
-        for r in range(S):
-            @pl.when(t == 2 + 2 * r)
-            def _():
-                vcopy(r).start()
-        for p in range(NP):
-            c = t - 1 - 2 * p
-            @pl.when((c >= 0) & (c < C))
-            def _():
-                finish(p, c)
-        for r in range(S):
-            @pl.when(t == 3 + 2 * r)
-            def _():
-                cp = vcopy(r)
-                cp.wait()
-                vbuf[r + 1] = vbuf[r] + vrecv[r]
-        return 0
-    lax.fori_loop(0, C + 2 * (NP - 1) + 1, step, 0)
-    vec_out[...] = vbuf[S]
-
-def all_reduce(parts, vec, dp_size, bucket_size, colours=False):
-    dims = bit_dims(dp_size, bucket_size)
-    S = len(dims)
-    width = parts[0].shape[1]
-    rows = sum(p.size for p in parts) // width
-    nblk = rows // width
-    CH = 8 << S
-    f32 = jnp.float32
-    any_spec = pl.BlockSpec(memory_space=pl.ANY)
-    vm = pl.BlockSpec(memory_space=pltpu.VMEM)
-    return pl.pallas_call(
-        functools.partial(ar_kernel, dims, nblk, colours),
-        out_shape=(jax.ShapeDtypeStruct((rows, width), f32), jax.ShapeDtypeStruct(vec.shape, f32)),
-        in_specs=[any_spec] * 6 + [vm], out_specs=(any_spec, vm),
-        scratch_shapes=[pltpu.VMEM((rows, width), f32)]
-        + [pltpu.VMEM((rows >> (s + 1), width), f32) for s in range(S)]
-        + [pltpu.VMEM((S + 1,) + vec.shape, f32), pltpu.VMEM((S,) + vec.shape, f32),
-           pltpu.SemaphoreType.DMA((nblk,)), pltpu.SemaphoreType.DMA((2 * S, rows // CH)), pltpu.SemaphoreType.DMA((2 * S, rows // CH)),
-           pltpu.SemaphoreType.DMA((rows // CH,)), pltpu.SemaphoreType.DMA((S,)), pltpu.SemaphoreType.DMA((S,)),
-           pltpu.SemaphoreType.REGULAR((S, rows // CH))],
-        compiler_params=pltpu.CompilerParams(collective_id=1, has_side_effects=True, vmem_limit_bytes=67043328),
-    )(*parts, vec)
 
 
 cos_scale = 20.0
@@ -485,11 +350,492 @@
     )(pool, sid, pair_order.reshape(1, -1), pair_order.reshape(-1, 1))
 
 
+UNIT = 256
+
+
 def norm_grad(dx, z, rate, gain):
     dz = dx * gain
     mean = jnp.mean(dz, axis=-1, keepdims=True)
     cross = jnp.mean(dz * z, axis=-1, keepdims=True)
-    return rate * (dz - mean - z * cross), jnp.sum(dx * z, axis=0), jnp.sum(dx, axis=0)
+    dh = rate * (dz - mean - z * cross)
+    return dh, jnp.sum(dx * z, axis=0, keepdims=True), jnp.sum(dx, axis=0, keepdims=True)
+
+
+def backward_kernel(
+    dims,
+    x_h, cot_h, q_h, k_h, v_h, c_h, nb_h, z1_h, r1_h, act_h, dg_h, z2_h, r2_h,
+    wq_h, wk_h, wv_h, wo_h, wi_h, w2_h,
+    lse, seg_row, seg_col, dpool, g1, g2,
+    tok_o, douter_o, dinner_o, dout_o, dq_o, dk_o, dv_o, vec_o,
+    grads, *rest,
+):
+    S = len(dims)
+    land, rest = rest[:S], rest[S:]
+    (
+        b0, b1, b2, b3, b4, b5, b6, b7, b8, b9, b10, grad, rbuf, bias, vbuf, vrecv,
+        lsem, ssem, rsem, osem, vs, vr, freed, slot, tsem,
+    ) = rest
+    total, width = grads.shape
+    rows = x_h.shape[0]
+    nrow = seg_row.shape[0]
+    seqlen = rows // nrow
+    pairs = width // 128
+    nff = w2_h.shape[0] // width
+    TM = 256
+    CH = 8 << S
+    C = total // CH
+    NS = land[0].shape[0] // (CH // 2)
+    M = CH // UNIT
+    route = Route(dims)
+    bar = pltpu.get_barrier_semaphore()
+
+    def plain(k):
+        axis, bit = dims[k]
+        where = list(route.pos)
+        where[axis] = where[axis] + bit * (1 - 2 * route.bits[k])
+        return tuple(where)
+
+    for k in range(S):
+        pl.semaphore_signal(bar, inc=1, device_id=plain(k), device_id_type=MESH)
+
+    def tile(i, size=TM):
+        return pl.ds(pl.multiple_of(i * size, size), size)
+
+    square = pl.ds(0, width)
+
+    def load(i, src, dst):
+        return pltpu.make_async_copy(src, dst, lsem.at[i])
+
+    def columns(j):
+        return pl.ds(pl.multiple_of(j * width, width), width)
+
+    def l_act(j):
+        return load(j, act_h.at[:, columns(j)], b0)
+
+    def l_dg(j):
+        return load(nff + j, dg_h.at[:, columns(j)], b1)
+
+    def l_w2(j):
+        return load(2 * nff + j, w2_h.at[columns(j)], b2.at[square])
+
+    def l_wi(j):
+        return load(3 * nff + j, wi_h.at[:, columns(j)], b3.at[square])
+
+    n = 4 * nff
+    l_cot = load(n, cot_h, b7)
+    l_z2 = load(n + 1, z2_h, b8)
+    l_r2 = load(n + 2, r2_h, rbuf)
+    l_nb = load(n + 3, nb_h, b5)
+    l_q = load(n + 4, q_h, b7)
+    l_k = load(n + 5, k_h, b8)
+    l_v = load(n + 6, v_h, b9)
+    l_wo = load(n + 7, wo_h, b10.at[square])
+    l_r1 = load(n + 8, r1_h, rbuf)
+    l_z1 = load(n + 9, z1_h, b0)
+    l_c = load(n + 10, c_h, b6)
+    l_x = load(n + 11, x_h, b5)
+    l_wq = load(n + 12, wq_h, b7.at[square])
+    l_wk = load(n + 13, wk_h, b8.at[square])
+    l_wv = load(n + 14, wv_h, b9.at[square])
+
+    for c in (l_cot, l_z2, l_r2, l_act(0), l_w2(0), l_dg(0), l_nb, l_wi(0), l_v, l_wo):
+        c.start()
+
+    DQB, DVB, DOB, DNG, DNS, DIB = 0, 1, 2, 3, 4, 5
+    D2B, DFG, DFS = DIB + nff, DIB + nff + 1, DIB + nff + 2
+    vbuf[...] = jnp.zeros_like(vbuf)
+
+    def vadd(i, value):
+        vbuf[0, pl.ds(i, 1)] = vbuf[0, pl.ds(i, 1)] + value
+
+    def second():
+        kinds = lax.broadcasted_iota(jnp.int32, (S_ROW, seqlen), 0)
+        for r in range(nrow):
+            onehot = (seg_row[r] == kinds).astype(F32)
+            count = jnp.sum(onehot, axis=1, keepdims=True)
+            share = dpool[r * S_ROW : (r + 1) * S_ROW] / count
+            grad[pl.ds(r * seqlen, seqlen)] = dot(onehot, share, 0, 0, HIGH)
+        l_cot.wait()
+        l_z2.wait()
+        l_r2.wait()
+
+        def body(i, _):
+            dx = b7[tile(i)].astype(F32) + grad[tile(i)]
+            dh, dg, db = norm_grad(dx, b8[tile(i)].astype(F32), rbuf[tile(i), 0:1], g2[...])
+            grad[tile(i)] = dh
+            b4[tile(i)] = dh.astype(BF)
+            vadd(DFG, dg)
+            vadd(DFS, db)
+            vadd(D2B, jnp.sum(dh, axis=0, keepdims=True))
+            return 0
+
+        lax.fori_loop(0, rows // TM, body, 0)
+        l_q.start()
+        l_k.start()
+        l_r1.start()
+
+    def outer(left, right, block):
+        def body(i, _):
+            cols = pl.ds(pl.multiple_of(i * TM, TM), TM)
+            at = pl.multiple_of(block * width + i * TM, TM)
+            grads[pl.ds(at, TM)] = dot(left[:, cols], right[...], 0, 0)
+            return 0
+
+        lax.fori_loop(0, width // TM, body, 0)
+
+    def ffn_outer(j):
+        l_act(j).wait()
+        outer(b0, b4, 2 * j)
+
+        @pl.when(j < nff - 1)
+        def _():
+            l_act(j + 1).start()
+
+        @pl.when(j == nff - 1)
+        def _():
+            l_z1.start()
+
+    def ffn_inner(j):
+        l_w2(j).wait()
+        l_dg(j).wait()
+
+        def body(i, _):
+            gi = dot(b4[tile(i)], b2[square], 1, 1) * b1[tile(i)].astype(F32)
+            b6[tile(i)] = gi.astype(BF)
+            vadd(DIB + j, jnp.sum(gi, axis=0, keepdims=True))
+            return 0
+
+        lax.fori_loop(0, rows // TM, body, 0)
+
+        @pl.when(j < nff - 1)
+        def _():
+            l_w2(j + 1).start()
+            l_dg(j + 1).start()
+
+    def ffn_dinner(j):
+        @pl.when(j == 0)
+        def _():
+            l_nb.wait()
+
+        outer(b5, b6, 2 * j + 1)
+
+        @pl.when(j == nff - 1)
+        def _():
+            l_x.start()
+
+    def ffn_back(j):
+        l_wi(j).wait()
+
+        def body(i, _):
+            grad[tile(i)] = grad[tile(i)] + dot(b6[tile(i)], b3[square], 1, 1)
+            return 0
+
+        lax.fori_loop(0, rows // TM, body, 0)
+
+        @pl.when(j < nff - 1)
+        def _():
+            l_wi(j + 1).start()
+
+        @pl.when(j == nff - 1)
+        def _():
+            l_c.start()
+
+    def first():
+        l_z1.wait()
+        l_r1.wait()
+
+        def body(i, _):
+            dh, dg, db = norm_grad(grad[tile(i)], b0[tile(i)].astype(F32), rbuf[tile(i), 0:1], g1[...])
+            grad[tile(i)] = dh
+            b4[tile(i)] = dh.astype(BF)
+            vadd(DNG, dg)
+            vadd(DNS, db)
+            vadd(DOB, jnp.sum(dh, axis=0, keepdims=True))
+            return 0
+
+        lax.fori_loop(0, rows // TM, body, 0)
+
+    def project():
+        l_c.wait()
+        l_wo.wait()
+        outer(b6, b4, 2 * nff)
+
+        def body(i, _):
+            b3[tile(i)] = dot(b4[tile(i)], b10[square], 1, 1).astype(BF)
+            return 0
+
+        lax.fori_loop(0, rows // TM, body, 0)
+        l_q.wait()
+        l_k.wait()
+        l_v.wait()
+
+    parts = halves()
+
+    def attention(a):
+        r = a // (pairs // 2)
+        span = tile(r, seqlen)
+        bias[...] = jnp.where(seg_col[span] == seg_row[r], 0.0, masked_score).astype(F32)
+
+        def pair(i, _):
+            p = (a - r * (pairs // 2)) * 2 + i
+            lanes = pl.ds(pl.multiple_of(p * 128, 128), 128)
+            qp = b7[span, lanes] * jnp.asarray(0.125, BF)
+            kp = b8[span, lanes]
+            vp = b9[span, lanes]
+            dc = b3[span, lanes]
+            dq = dk = dv = 0.0
+            for half, part in enumerate(parts):
+                k1 = kp * part
+                s = dot(k1, qp, 1, 1) + bias[...]
+                prob = jnp.exp(s - lse[(r * pairs + p) * 2 + half])
+                dp = dot(vp * part, dc, 1, 1)
+                dv = dv + dot(prob.astype(BF), dc * part, 1, 0)
+                mean = jnp.sum(prob * dp, axis=0, keepdims=True)
+                ds = (prob * (dp - mean)).astype(BF)
+                dk = dk + dot(ds, qp * part, 1, 0)
+                dq = dq + dot(k1, ds, 0, 0)
+            dq = 0.125 * dq.T
+            b0[span, lanes] = dq.astype(BF)
+            b1[span, lanes] = dk.astype(BF)
+            b2[span, lanes] = dv.astype(BF)
+            vbuf[0, DQB : DQB + 1, lanes] = vbuf[0, DQB : DQB + 1, lanes] + jnp.sum(dq, axis=0, keepdims=True)
+            vbuf[0, DVB : DVB + 1, lanes] = vbuf[0, DVB : DVB + 1, lanes] + jnp.sum(dv, axis=0, keepdims=True)
+            return 0
+
+        lax.fori_loop(0, 2, pair, 0)
+
+    def token_part(i):
+        out = grad[tile(i)] + dot(b0[tile(i)], b7[square], 1, 1)
+        out = out + dot(b1[tile(i)], b8[square], 1, 1)
+        grad[tile(i)] = out + dot(b2[tile(i)], b9[square], 1, 1)
+
+    T_LN = 4 * nff - 1
+    A0 = T_LN + 2
+    A1 = A0 + nrow * pairs // 2
+    T_TOK = A1 + 3
+    T_END = T_TOK + rows // TM
+
+    def slices(t):
+        u = t + 1
+        j = u // 4
+
+        for kind, work in enumerate((ffn_outer, ffn_inner, ffn_dinner, ffn_back)):
+            @pl.when((u < 4 * nff) & (u - 4 * j == kind))
+            def _():
+                work(j)
+
+        pl.when(t == T_LN)(first)
+        pl.when(t == T_LN + 1)(project)
+
+        @pl.when((t >= A0) & (t < A1))
+        def _():
+            attention(t - A0)
+
+        @pl.when(t == A1)
+        def _():
+            l_wq.start()
+            l_wk.start()
+            l_wv.start()
+            l_x.wait()
+
+        for i, src in enumerate((b0, b1, b2)):
+            @pl.when(t == A1 + i)
+            def _():
+                outer(b5, src, 2 * nff + 1 + i)
+
+        @pl.when(t == T_TOK)
+        def _():
+            l_wq.wait()
+            l_wk.wait()
+            l_wv.wait()
+
+        @pl.when((t >= T_TOK) & (t < T_END))
+        def _():
+            token_part(t - T_TOK)
+
+        @pl.when(t == T_END)
+        def _():
+            pltpu.make_async_copy(grad, tok_o, tsem).start()
+
+    def offset(s, c):
+        o = c * CH
+        for k in range(s):
+            o = o + route.bit(k, colour_of(c)) * (CH >> (k + 1))
+        return o
+
+    def reduce_copy(s, c):
+        half = CH >> (s + 1)
+        b = route.bit(s, colour_of(c))
+        o = offset(s, c)
+        keep = pl.multiple_of(o + b * half, 8)
+        send = pl.multiple_of(o + (1 - b) * half, 8)
+        here = pl.multiple_of((c % NS) * half, 8)
+        cp = pltpu.make_async_remote_copy(
+            grads.at[pl.ds(send, half)], land[s].at[pl.ds(here, half)],
+            ssem.at[s, c], rsem.at[s, c],
+            device_id=route.partner(s, colour_of(c)), device_id_type=MESH,
+        )
+        return cp, keep, here, half
+
+    def gather_copy(s, c):
+        half = CH >> (s + 1)
+        keep = pl.multiple_of(offset(s, c) + route.bit(s, colour_of(c)) * half, 8)
+        rank = 2 * S - 1 - s
+        return pltpu.make_async_remote_copy(
+            grads.at[pl.ds(keep, half)], grads.at[pl.ds(keep, half)],
+            ssem.at[rank, c], rsem.at[rank, c],
+            device_id=route.partner(s, colour_of(c)), device_id_type=MESH,
+        )
+
+    per = width // UNIT
+
+    def out_copies(c, start):
+        for i in range(M):
+            unit = c * M + i
+            src = grads.at[pl.ds(pl.multiple_of(unit * UNIT, UNIT), UNIT)]
+            if not start:
+                pltpu.make_async_copy(src, dq_o.at[pl.ds(0, UNIT)], osem.at[unit]).wait()
+                continue
+            block = unit // per
+            line = pl.multiple_of((unit - block * per) * UNIT, UNIT)
+            for b in range(2 * nff + 4):
+                if b >= 2 * nff:
+                    dst = (dout_o, dq_o, dk_o, dv_o)[b - 2 * nff].at[pl.ds(line, UNIT)]
+                elif b % 2 == 0:
+                    dst = douter_o.at[pl.ds(b // 2 * width + line, UNIT)]
+                else:
+                    dst = dinner_o.at[pl.ds(line, UNIT), pl.ds(b // 2 * width, width)]
+
+                @pl.when(block == b)
+                def _():
+                    pltpu.make_async_copy(src, dst, osem.at[unit]).start()
+
+    def start(p, c):
+        if p < S:
+            @pl.when(c >= NS)
+            def _():
+                pl.semaphore_wait(slot.at[p, c], 1)
+
+            reduce_copy(p, c)[0].start()
+        elif p < 2 * S:
+            s = 2 * S - 1 - p
+            pl.semaphore_wait(freed.at[s, c], 1)
+            gather_copy(s, c).start()
+        else:
+            out_copies(c, True)
+
+    def finish(p, c):
+        if p < S:
+            cp, keep, here, half = reduce_copy(p, c)
+            cp.wait_recv()
+            grads[pl.ds(keep, half)] = grads[pl.ds(keep, half)] + land[p][pl.ds(here, half)]
+            cp.wait_send()
+            pl.semaphore_signal(
+                freed.at[p, c], inc=1, device_id=route.partner(p, colour_of(c)), device_id_type=MESH
+            )
+
+            @pl.when(c + NS < C)
+            def _():
+                pl.semaphore_signal(
+                    slot.at[p, c + NS], inc=1,
+                    device_id=route.partner(p, colour_of(c + NS)), device_id_type=MESH,
+                )
+        elif p < 2 * S:
+            gather_copy(2 * S - 1 - p, c).wait()
+        else:
+            out_copies(c, False)
+
+    def vec_copy(r):
+        return pltpu.make_async_remote_copy(
+            vbuf.at[r], vrecv.at[r], vs.at[r], vr.at[r], device_id=plain(r), device_id_type=MESH
+        )
+
+    NP = 2 * S + 1
+
+    def at(t, p):
+        if M == 1:
+            c = t - 2 * p
+            return c, (c >= 0) & (c < C)
+        c = (t - 2 * p + 1) // M - 1
+        return c, (c >= 0) & (c < C) & ((c + 1) * M == t - 2 * p + 1)
+
+    def step(t, _):
+        for p in range(NP):
+            c, valid = at(t, p)
+            pl.when(valid)(functools.partial(start, p, c))
+        for r in range(S):
+            @pl.when(t == T_TOK + 2 * r)
+            def _():
+                vec_copy(r).start()
+        slices(t)
+        for p in range(NP):
+            c, valid = at(t - 1, p)
+            pl.when(valid)(functools.partial(finish, p, c))
+        for r in range(S):
+            @pl.when(t == T_TOK + 1 + 2 * r)
+            def _():
+                cp = vec_copy(r)
+                cp.wait()
+                vbuf[r + 1] = vbuf[r] + vrecv[r]
+        return 0
+
+    second()
+    ffn_outer(0)
+    pl.semaphore_wait(bar, S)
+    steps = max(C * M + 2 * (NP - 1) + 1, T_TOK + 2 * S, T_END + 1)
+    lax.fori_loop(0, steps, step, 0)
+    pltpu.make_async_copy(grad, tok_o, tsem).wait()
+    vec_o[...] = vbuf[S]
+
+
+def backward_reduce(
+    tokens, cotangent, kept, weights, lse, segment, dpooled, g1, g2, dp_size, bucket_size
+):
+    rows, width = tokens.shape
+    nrow, seqlen = segment.shape
+    wq, wk, wv, wo, wi, w2 = weights
+    inner = wi.shape[1]
+    nff = inner // width
+    dims = bit_dims(dp_size, bucket_size)
+    S = len(dims)
+    CH = 8 << S
+    total = (2 * nff + 4) * width
+    C = total // CH
+    NS = max(2, 2048 // CH)
+    nvec = -(-(8 + nff) // 8) * 8
+    vm = pl.BlockSpec(memory_space=pltpu.VMEM)
+    hbm = pl.BlockSpec(memory_space=pl.ANY)
+    sd = jax.ShapeDtypeStruct
+    dma = pltpu.SemaphoreType.DMA
+    plain = pltpu.SemaphoreType.REGULAR
+    full = sd((width, width), F32)
+    row = lambda a: a.reshape(1, -1)
+    return pl.pallas_call(
+        functools.partial(backward_kernel, dims),
+        name="backward_reduce",
+        out_shape=(
+            sd((rows, width), F32), sd((inner, width), F32), sd((width, inner), F32),
+            full, full, full, full, sd((nvec, width), F32),
+        ),
+        in_specs=[hbm] * 19 + [vm] * 6,
+        out_specs=[hbm] * 7 + [vm],
+        scratch_shapes=[pltpu.VMEM((total, width), F32)]
+        + [pltpu.VMEM((NS * (CH >> (s + 1)), width), F32) for s in range(S)]
+        + [pltpu.VMEM((rows, width), BF)] * 11
+        + [
+            pltpu.VMEM((rows, width), F32), pltpu.VMEM((rows, 128), F32),
+            pltpu.VMEM((seqlen, seqlen), F32), pltpu.VMEM((S + 1, nvec, width), F32),
+            pltpu.VMEM((S, nvec, width), F32),
+            dma((4 * nff + 15,)), dma((2 * S, C)), dma((2 * S, C)), dma((total // UNIT,)),
+            dma((S,)), dma((S,)), plain((S, C)), plain((S, C)), dma,
+        ],
+        compiler_params=pltpu.CompilerParams(
+            collective_id=1, has_side_effects=True, vmem_limit_bytes=67043328
+        ),
+    )(
+        tokens, cotangent, *kept, wq, wk, wv, wo, wi, w2, lse,
+        segment.reshape(nrow, 1, seqlen), segment.reshape(rows, 1), dpooled, row(g1), row(g2),
+    )
 
 
 def local(
@@ -498,7 +844,6 @@
     value_bias, out_weight, out_bias, norm_gain, norm_shift, inner_weight, inner_bias,
     outer_weight, outer_bias, final_gain, final_shift,
 ):
-    nrows, seqlen = segment.shape
     width = tokens.shape[1]
     (
         query_b, key_b, value_b, context_b, normed_b, z1, r1, active_b, slope, z2, r2, lse,
@@ -510,78 +855,19 @@
     )
     dpooled, loss_value = pair_loss(pooled, pair_order, dp_size, bucket_size)
     loss_value = loss_value.reshape(())
-    onehot = (segment[:, None, :] == jnp.arange(S_ROW, dtype=jnp.int32)[None, :, None]).astype(F32)
-    counts = jnp.sum(onehot, axis=2, keepdims=True)
-    spread = jnp.einsum(
-        "rsl,rsd->rld", onehot, dpooled.reshape(nrows, S_ROW, width) / counts, precision=HIGH
+    kept = (
+        query_b, key_b, value_b, context_b, normed_b, z1, r1, active_b, slope, z2, r2,
     )
-    grad_final = cotangent.astype(F32) + spread.reshape(nrows * seqlen, width)
-    grad_second, dfinal_gain, dfinal_shift = norm_grad(
-        grad_final, z2.astype(F32), r2[:, :1], final_gain
+    weights = (query_weight, key_weight, value_weight, out_weight, inner_weight, outer_weight)
+    (
+        tokens_grad, douter_weight, dinner_weight, dout_weight, dquery_weight, dkey_weight,
+        dvalue_weight, packed,
+    ) = backward_reduce(
+        tokens, cotangent, kept, weights, lse, segment, dpooled, norm_gain, final_gain,
+        dp_size, bucket_size,
     )
-    grad_second_b = grad_second.astype(BF)
-    douter_weight = dot(active_b, grad_second_b, 0, 0)
-    douter_bias = jnp.sum(grad_second, axis=0)
-    grad_inner = dot(grad_second_b, outer_weight, 1, 1) * slope.astype(F32)
-    grad_inner_b = grad_inner.astype(BF)
-    dinner_weight = dot(normed_b, grad_inner_b, 0, 0)
-    dinner_bias = jnp.sum(grad_inner, axis=0)
-    grad_normed = grad_second + dot(grad_inner_b, inner_weight, 1, 1)
-    grad_first, dnorm_gain, dnorm_shift = norm_grad(
-        grad_normed, z1.astype(F32), r1[:, :1], norm_gain
-    )
-    grad_first_b = grad_first.astype(BF)
-    dout_weight = dot(context_b, grad_first_b, 0, 0)
-    dout_bias = jnp.sum(grad_first, axis=0)
-    split = lambda a: a.reshape(nrows, seqlen, H, HD)
-    grad_context = split(dot(grad_first_b, out_weight, 1, 1).astype(BF))
-    query_h, key_h, value_h = split(query_b), split(key_b), split(value_b)
-    same = segment[:, None, :, None] == segment[:, None, None, :]
-    ein = functools.partial(jnp.einsum, preferred_element_type=F32)
-    scores = jnp.where(same, ein("rqhe,rkhe->rhqk", query_h, key_h) * 0.125, masked_score)
-    probs = jnp.exp(scores - lse.reshape(nrows, H, seqlen, 1))
-    probs_b = probs.astype(BF)
-    grad_probs = ein("rqhe,rkhe->rhqk", grad_context, value_h)
-    grad_value = ein("rhqk,rqhe->rkhe", probs_b, grad_context)
-    grad_scores = probs * (grad_probs - jnp.sum(probs * grad_probs, axis=-1, keepdims=True))
-    grad_scores_b = grad_scores.astype(BF)
-    grad_query = ein("rhqk,rkhe->rqhe", grad_scores_b, key_h) * 0.125
-    grad_key = ein("rhqk,rqhe->rkhe", grad_scores_b, query_h) * 0.125
-    grad_query = grad_query.reshape(nrows * seqlen, width)
-    grad_key = grad_key.reshape(nrows * seqlen, width)
-    grad_value = grad_value.reshape(nrows * seqlen, width)
-    dquery_bias = jnp.sum(grad_query, axis=0)
-    dvalue_bias = jnp.sum(grad_value, axis=0)
-    grad_query_b = grad_query.astype(BF)
-    grad_key_b = grad_key.astype(BF)
-    grad_value_b = grad_value.astype(BF)
-    dquery_weight = dot(tokens, grad_query_b, 0, 0)
-    dkey_weight = dot(tokens, grad_key_b, 0, 0)
-    dvalue_weight = dot(tokens, grad_value_b, 0, 0)
-    tokens_grad = (
-        grad_first
-        + dot(grad_query_b, query_weight, 1, 1)
-        + dot(grad_key_b, key_weight, 1, 1)
-        + dot(grad_value_b, value_weight, 1, 1)
-    )
-    vectors = [
-        dquery_bias, dvalue_bias, dout_bias, dnorm_gain, dnorm_shift,
-        dinner_bias, douter_bias, dfinal_gain, dfinal_shift,
-    ]
-    packed = jnp.concatenate(vectors).reshape(-1, width)
-    nvec = packed.shape[0]
-    packed = jnp.pad(packed, ((0, -nvec % 8), (0, 0)))
-    flat, packed = all_reduce(
-        [douter_weight, dinner_weight, dout_weight, dquery_weight, dkey_weight, dvalue_weight],
-        packed, dp_size, bucket_size, True,
-    )
-    blocks = flat.reshape(-1, width, width)
-    wide = inner_weight.shape[1] // width
-    douter_weight = flat[: wide * width]
-    dinner_weight = jnp.concatenate([blocks[wide + j] for j in range(wide)], axis=1)
-    dout_weight, dquery_weight, dkey_weight, dvalue_weight = (blocks[2 * wide + j] for j in range(4))
-    packed = packed[:nvec].reshape(-1)
-    sizes = [v.shape[0] for v in vectors]
+    packed = packed.reshape(-1)
+    sizes = [width] * 5 + [inner_bias.shape[0]] + [width] * 3
     ends = [sum(sizes[: i + 1]) for i in range(len(sizes))]
     (
         dquery_bias, dvalue_bias, dout_bias, dnorm_gain, dnorm_shift,

time: 580 us -> 387 us (0.67); the launches traced: 569 us -> 387 us
  matrix products: 130 us -> 0 us
  other arithmetic: 33.8 us -> 0.01 us
  local copies, waits for them, and re-layouts: 72.4 us -> 40.6 us
  Pallas kernels: 330 us -> 344 us
    dot_general x18 -> x0, matrix products: 130 us -> none  [the longest x12 68.2 us: dot(): lax.dot_general(a, b, (((da,), (db,)), ((), ())), precision=precision, pr...]
    convert_element_type x1 -> x0, other arithmetic: 21.5 us -> none  [local(): grad_scores_b = grad_scores.astype(BF)]
    slice x3 -> x0, local copies, waits for them, and re-layouts: 20.5 us -> none  [the longest x1 10.9 us: local(): blocks[wide + j]]
    unnamed x69 -> x29, local copies, waits for them, and re-layouts: 7.21 us -> 24.5 us
    pallas_call x1, Pallas kernels: 246 us -> 260 us  [backward_reduce(): pl.pallas_call(functools.partial(backward_kernel, dims), name='backward_r...]
    reshape x5 -> x0, local copies, waits for them, and re-layouts: 12 us -> none  [the longest x4 12 us: local(): split = lambda a: a.reshape(nrows, seqlen, H, HD)]
    convert_element_type x4 -> x0, local copies, waits for them, and re-layouts: 8.99 us -> none  [the longest x1 3.18 us: local(): grad_value_b = grad_value.astype(BF)]
    pallas_call x3 -> x0, local copies, waits for them, and re-layouts: 6.89 us -> none  [forward(): pl.pallas_call(forward_kernel, name='forward', out_shape=outs, in_specs=[...]
where the time goes in v3:
time: 387 us
  Pallas kernels  344 us (89%)
  local copies, waits for them, and re-layouts  40.6 us (10%)
    pallas_call x1, Pallas kernels, backward_reduce(): pl.pallas_call(functools.partial(backward_kernel, dims), name='backward_r...  260 us
    pallas_call x1, Pallas kernels, forward(): pl.pallas_call(forward_kernel, name='forward', out_shape=outs, in_specs=[...  50 us
    pallas_call x1, Pallas kernels, pair_loss(): pl.pallas_call(functools.partial(loss_kernel, dims, bucket_size), name='p...  34.3 us
    unnamed x29, local copies, waits for them, and re-layouts  24.5 us
    reshape x8, local copies, waits for them, and re-layouts, forward(): row = lambda a: a.reshape(1, -1)  10.1 us

profile of v3, /device:TPU:0, one launch (start us, length us, event | category | flops | bytes accessed | tf_op | source)
XLA Modules:
  0.0 386.8 jit_solution(7193072733551050151)
XLA Ops:
  0.7 1.3 reshape.97.g1
  1.9 1.3 reshape.101.g2
  3.2 1.3 reshape.94.bq
  4.5 1.3 reshape.95.bv
  5.7 1.3 reshape.96.bo
  7.0 1.3 reshape.98.s1
  8.3 1.3 reshape.100.b2
  9.5 1.3 reshape.102.s2
  10.8 1.3 reshape.92.seg_row
  12.1 0.7 copy.41
  12.8 1.5 copy.39.pair_col
  14.3 1.0 copy.42
  15.3 50.0 %forward.1 = (bf16[1024,768]{1,0:T(8,128)(2,1)}, bf16[1024,768]{1,0:T(8,128)(2,1)}, bf16[1024,768]{1,0:T(8,128)(2,1)}, bf16[1024,768]{1,0:T(8,128)(2,1)}, bf16[1...) custom-call(bf16[1024,768]{1,0:T(8,128)(2,1)} %x_h.1, ...), custom_call_target="tpu_custom_call" | custom-call | tf_op jit(solution)/shard_map/forward/pallas_call | solution.py:186
  65.3 34.3 %pair_loss.1 = (f32[16,768]{1,0:T(8,128)}, f32[1,1]{1,0:T(1,128)}) custom-call(f32[16,768]{1,0:T(8,128)} %get-tuple-element.43.pool, s32[1,512]{1,0:T(1,128)} %constant.2.clone.sid, s32[1,512]{1,0:T(1,128)} %bitcast.18, s32[512,1]{1,0:T(8,128)} %copy.39.pair_col), custom_call_target="tpu_custom_call" | custom-call | tf_op jit(solution)/shard_map/pair_loss/pallas_call | solution.py:339
  99.6 259.6 %backward_reduce.1 = (f32[1024,768]{1,0:T(8,128)}, f32[3072,768]{1,0:T(8,128)}, f32[768,3072]{1,0:T(8,128)}, f32[768,768]{1,0:T(8,128)}, f32[768,768]{1,0:T(8,12...) custom-call(bf16[1024,768]{1,0:T(8,128)(2,1)} %x_h.1, bf16[1024,768]{1,0:T(8,128)(2,1)} %cot_h.1, ...), custom_call_target="tpu_custom_call" | custom-call | tf_op jit(solution)/shard_map/backward_reduce/pallas_call | solution.py:813
  359.2 0.8 slice.64
  360.0 0.0 copy-start.3
  360.0 1.7 slice_reduce_fusion
  361.6 0.6 slice.65
  362.8 0.0 copy-start.2
  362.8 0.0 slice-start.3
  362.8 3.9 %copy.52 = f32[1024,768]{1,0:T(8,128)} copy(f32[1024,768]{1,0:T(8,128)} %get-tuple-element.94) | data formatting | bytes 6291456
  366.7 0.0 copy-done.3
  366.7 0.0 slice-start.4
  366.8 1.4 copy.53
  368.2 0.0 copy-done.2
  368.2 0.0 copy-start.1
  368.2 1.4 copy.54
  369.6 1.8 copy-done.1
  371.4 0.0 copy-start
  371.4 0.0 slice-start.5
  371.4 1.4 copy.55
  372.8 1.1 copy-done
  373.9 0.0 slice-start
  373.9 1.4 copy.56
  375.3 0.0 slice-done.3
  375.3 0.0 slice-done.4
  375.3 0.0 slice-done.5
  375.3 0.0 slice-start.1
  375.3 0.0 slice-start.2
  375.3 4.8 %copy.57 = f32[768,3072]{1,0:T(8,128)} copy(f32[768,3072]{1,0:T(8,128)S(1)} %bitcast.11) | data formatting | bytes 18874368
  380.1 0.0 slice-done
  380.1 1.6 slice-done.1
  381.7 0.2 slice-done.2
  381.9 3.7 copy.58
  (2 shorter events, 0.0 us)
Async XLA Ops:
  360.0 6.8 %copy-start.3 = (f32[768,768]{1,0:T(8,128)S(1)}, f32[768,768]{1,0:T(8,128)}, u32[]{:S(2)}) copy-start(f32[768,768]{1,0:T(8,128)} %get-tuple-element.95) | copy-start | bytes 7077892
  362.8 5.3 %copy-start.2 = (f32[768,768]{1,0:T(8,128)S(1)}, f32[768,768]{1,0:T(8,128)}, u32[]{:S(2)}) copy-start(f32[768,768]{1,0:T(8,128)} %get-tuple-element.97) | copy-start | bytes 7077892
  362.8 12.5 %slice-start.3 = ((s8[9437184]{0:T(1024)(128)(4,1)}), s8[4194304]{0:T(1024)(128)(4,1)S(1)}, s32[]{:S(2)}) async-start(s8[9437184]{0:T(1024)(128)(4,1)} %bitcast.10), calls=%async_computation.3 | async-start | bytes 8388608
  366.7 8.6 %slice-start.4 = ((s8[9437184]{0:T(1024)(128)(4,1)}), s8[4194304]{0:T(1024)(128)(4,1)S(1)}, s32[]{:S(2)}) async-start(s8[9437184]{0:T(1024)(128)(4,1)} %bitcast.10), calls=%async_computation.4 | async-start | bytes 8388608
  368.2 3.2 copy-start.1
  371.4 2.5 copy-start
  371.4 3.9 %slice-start.5 = ((s8[9437184]{0:T(1024)(128)(4,1)}), s8[1048576]{0:T(1024)(128)(4,1)S(1)}, s32[]{:S(2)}) async-start(s8[9437184]{0:T(1024)(128)(4,1)} %bitcast.10), calls=%async_computation.5 | async-start | bytes 2097152
  373.9 6.2 %slice-start = ((s8[9437184]{0:T(1024)(128)(4,1)}), s8[4194304]{0:T(1024)(128)(4,1)S(1)}, s32[]{:S(2)}) async-start(s8[9437184]{0:T(1024)(128)(4,1)} %bitcast.8), calls=%async_computation | async-start | bytes 8388608
  375.3 6.4 %slice-start.1 = ((s8[9437184]{0:T(1024)(128)(4,1)}), s8[4194304]{0:T(1024)(128)(4,1)S(1)}, s32[]{:S(2)}) async-start(s8[9437184]{0:T(1024)(128)(4,1)} %bitcast.8), calls=%async_computation.1 | async-start | bytes 8388608
  375.3 6.6 %slice-start.2 = ((s8[9437184]{0:T(1024)(128)(4,1)}), s8[1048576]{0:T(1024)(128)(4,1)S(1)}, s32[]{:S(2)}) async-start(s8[9437184]{0:T(1024)(128)(4,1)} %bitcast.8), calls=%async_computation.2 | async-start | bytes 2097152

commit v4 on v3

--- a/solution.py
+++ b/solution.py
@@ -8,8 +8,6 @@
 from jax.experimental.pallas import tpu as pltpu
 from jax.sharding import PartitionSpec as P
 
-H = 12
-HD = 64
 S_ROW = 8
 norm_eps = 1e-05
 masked_score = -1000000000.0
@@ -30,6 +28,11 @@
     return low.astype(BF), (1.0 - low).astype(BF)
 
 
+def column(line):
+    tall = jnp.broadcast_to(line.astype(F32), (8, line.shape[1])).T
+    return tall[:, :1].astype(jnp.int32)
+
+
 def normalise(hidden):
     centred = hidden - jnp.mean(hidden, axis=-1, keepdims=True)
     rate = lax.rsqrt(jnp.mean(centred * centred, axis=-1, keepdims=True) + norm_eps)
@@ -37,13 +40,13 @@
 
 
 def forward_kernel(
-    x_in, seg_row, seg_col, wq_h, bq, wk_h, wv_h, bv, wo_h, bo, g1, s1, wi_h, bi, w2_h, b2, g2, s2,
+    x_in, seg, wq_h, bq, wk_h, wv_h, bv, wo_h, bo, g1, s1, wi_h, bi, w2_h, b2, g2, s2,
     q_o, k_o, v_o, c_o, nb_o, z1_o, r1_o, act_o, dg_o, z2_o, r2_o, lse_o, out_o, pool_o,
-    wq, wk, wv, wo, wi, w2, q, k, v, ctx, nf, nb, z1, r1, act, dg, z2, r2, fin, lout, bias,
+    wq, wk, wv, wo, wi, w2, q, k, v, ctx, nf, nb, z1, r1, act, dg, z2, r2, fin, lout, bias, flat,
     wsem, osem,
 ):
     rows, width = x_in.shape
-    nrow = seg_row.shape[0]
+    nrow = seg.shape[0]
     seqlen = rows // nrow
     pairs = width // 128
     inner = wi.shape[1]
@@ -56,6 +59,13 @@
     ]
     for c in loads:
         c.start()
+    row_refs = []
+    for i, a in enumerate((bq, bv, bo, g1, s1, b2, g2, s2)):
+        at = flat.at[pl.ds(i, 1), pl.ds(0, width)]
+        at[...] = a[...].reshape(1, -1)
+        row_refs.append(at)
+    bq, bv, bo, g1, s1, b2, g2, s2 = row_refs
+    flat[8:9] = bi[...].reshape(1, -1)
     stores = []
 
     def put(i, src, dst):
@@ -84,7 +94,8 @@
 
     def row(r, _):
         span = pl.ds(pl.multiple_of(r * seqlen, seqlen), seqlen)
-        same = seg_col[span] == seg_row[r]
+        line = seg[pl.ds(r, 1)]
+        same = column(line) == line
         bias[...] = jnp.where(same, 0.0, masked_score).astype(F32)
 
         def pair(p, _):
@@ -133,7 +144,7 @@
     def feed(i, _):
         def block(j, _):
             cols = pl.ds(pl.multiple_of(j * TF, TF), TF)
-            h = dot(nb[tile(i)], wi[:, cols], 1, 0) + bi[:, cols]
+            h = dot(nb[tile(i)], wi[:, cols], 1, 0) + flat[8:9, cols]
             cdf = 0.5 + 0.5 * lax.erf(h * 0.7071067811865476)
             act_b = (h * cdf).astype(BF)
             act[tile(i), cols] = act_b
@@ -159,7 +170,7 @@
     put(11, lout, out_o)
     for r in range(nrow):
         kinds = lax.broadcasted_iota(jnp.int32, (S_ROW, seqlen), 0)
-        onehot = (seg_row[r] == kinds).astype(F32)
+        onehot = (seg[r : r + 1] == kinds).astype(F32)
         count = jnp.sum(onehot, axis=1, keepdims=True)
         got = dot(onehot, fin[r * seqlen : (r + 1) * seqlen], 1, 0, HIGH)
         pool_o[r * S_ROW : (r + 1) * S_ROW] = got / count
@@ -182,12 +193,11 @@
         sd((rows, 128), F32), sd(wide, BF), sd(wide, BF), sd(act, BF), sd((rows, 128), F32),
         sd((nrow * heads, 1, seqlen), F32), sd(act, BF), sd((nrow * S_ROW, width), F32),
     )
-    row = lambda a: a.reshape(1, -1)
     return pl.pallas_call(
         forward_kernel,
         name="forward",
         out_shape=outs,
-        in_specs=[vm, vm, vm, hbm, vm, hbm, hbm, vm, hbm, vm, vm, vm, hbm, vm, hbm, vm, vm, vm],
+        in_specs=[vm, vm, hbm, vm, hbm, hbm, vm, hbm, vm, vm, vm, hbm, vm, hbm, vm, vm, vm],
         out_specs=[hbm] * 11 + [vm, hbm, vm],
         scratch_shapes=[pltpu.VMEM((width, width), BF)] * 4
         + [pltpu.VMEM((width, inner), BF), pltpu.VMEM((inner, width), BF)]
@@ -195,11 +205,11 @@
         + [pltpu.VMEM(act, F32), pltpu.VMEM(act, BF), pltpu.VMEM(act, BF), pltpu.VMEM((rows, 128), F32)]
         + [pltpu.VMEM(wide, BF), pltpu.VMEM(wide, BF), pltpu.VMEM(act, BF), pltpu.VMEM((rows, 128), F32)]
         + [pltpu.VMEM(act, F32), pltpu.VMEM(act, BF), pltpu.VMEM((seqlen, seqlen), F32)]
+        + [pltpu.VMEM((16, inner), F32)]
         + [pltpu.SemaphoreType.DMA((6,)), pltpu.SemaphoreType.DMA((12,))],
         compiler_params=pltpu.CompilerParams(vmem_limit_bytes=64000000),
     )(
-        tokens, segment.reshape(nrow, 1, seqlen), segment.reshape(rows, 1), wq, row(bq), wk, wv,
-        row(bv), wo, row(bo), row(g1), row(s1), wi, row(bi), w2, row(b2), row(g2), row(s2),
+        tokens, segment, wq, bq, wk, wv, bv, wo, bo, g1, s1, wi, bi, w2, b2, g2, s2,
     )
 
 
@@ -221,22 +231,17 @@
         self.bits = [(self.pos[a] // b) % 2 for a, b in dims]
 
     def weights(self, stage, colour=0):
-        core = self.bits[0]
         n = len(self.dims)
         if stage == 0 or n < 3:
             return {stage: 1}
-        if n != 5 or isinstance(colour, int):
-            if stage in (1, 2):
-                return {stage: 1 - core, 3 - stage: core}
-            return {stage: 1}
-        keep = 1 - colour
-        table = {
-            1: {1: keep * (1 - core), 2: keep * core, 3: colour},
-            2: {2: keep * (1 - core), 1: keep * core, 4: colour},
-            3: {3: keep, 1: colour * (1 - core), 2: colour * core},
-            4: {4: keep, 2: colour * (1 - core), 1: colour * core},
-        }
-        return table[stage]
+        order = list(range(n))
+        if colour:
+            order = [0] + order[3:] + [1, 2]
+        d = order[stage]
+        if d in (1, 2):
+            core = self.bits[0]
+            return {d: 1 - core, 3 - d: core}
+        return {d: 1}
 
     def bit(self, stage, colour=0):
         w = self.weights(stage, colour)
@@ -248,9 +253,6 @@
             axis, bit = self.dims[k]
             where[axis] = where[axis] + v * (bit * (1 - 2 * self.bits[k]))
         return tuple(where)
-
-def colour_of(c):
-    return 1 - ((2 * c) % 9 + 7) // 9
 
 
 cos_scale = 20.0
@@ -275,12 +277,14 @@
     return vectors * factor, factor
 
 
-def loss_kernel(dims, bucket_size, pool, sid, pair_row, pair_col, dpool, loss, buf, unit, weigh, ssem, rsem):
+def loss_kernel(dims, bucket_size, pool, sid, order, dpool, loss, buf, unit, weigh, tall, ssem, rsem):
     own, width = pool.shape
     sents = buf.shape[0]
     pairs = sents // 2
     S = len(dims)
     route = Route(dims)
+    pair_row = order[...].reshape(1, -1)
+    tall[...] = jnp.broadcast_to(column(pair_row), tall.shape)
     bar = pltpu.get_barrier_semaphore()
     for k in range(S):
         axis, bit = dims[k]
@@ -304,7 +308,7 @@
     B = min(256, pairs)
     for i in range(sents // B):
         part = pl.ds(i * B, B)
-        pick = (pair_col[part] == sid[...]).astype(F32)
+        pick = (tall[part, 0:1] == sid[...]).astype(F32)
         ordered = dot(pick, buf[...], 1, 0, HIGH)
         unit[part] = sphere(ordered)[0]
     total = jnp.zeros((1, 1), F32)
@@ -321,7 +325,7 @@
     loss[...] = total
     first = (route.pos[0] * bucket_size + route.pos[1]) * own
     mine = lax.broadcasted_iota(jnp.int32, (own, sents), 0) + first
-    choose = (mine == pair_row[...]).astype(F32)
+    choose = (mine == pair_row).astype(F32)
     by_row = dot(choose[:, :pairs], weigh[...], 1, 0, HIGH)
     by_column = dot(choose[:, pairs:], weigh[...], 1, 1, HIGH)
     grad = cos_scale * (dot(by_row, unit[pairs:], 1, 0, HIGH) + dot(by_column, unit[:pairs], 1, 0, HIGH))
@@ -340,17 +344,20 @@
         functools.partial(loss_kernel, dims, bucket_size),
         name="pair_loss",
         out_shape=(jax.ShapeDtypeStruct(pool.shape, F32), jax.ShapeDtypeStruct((1, 1), F32)),
-        in_specs=[vm] * 4, out_specs=(vm, vm),
+        in_specs=[vm] * 3, out_specs=(vm, vm),
         scratch_shapes=[
             pltpu.VMEM((sents, width), F32), pltpu.VMEM((sents, width), F32),
-            pltpu.VMEM((sents // 2, sents // 2), F32),
+            pltpu.VMEM((sents // 2, sents // 2), F32), pltpu.VMEM((sents, 128), jnp.int32),
             pltpu.SemaphoreType.DMA((S,)), pltpu.SemaphoreType.DMA((S,)),
         ],
         compiler_params=pltpu.CompilerParams(collective_id=2, has_side_effects=True, vmem_limit_bytes=60000000),
-    )(pool, sid, pair_order.reshape(1, -1), pair_order.reshape(-1, 1))
-
-
-UNIT = 256
+    )(pool, sid, pair_order)
+
+
+NARROW = 128
+VMEM_KERNEL = 33800000
+LAG = 2
+FIN = 1
 
 
 def norm_grad(dx, z, rate, gain):
@@ -365,19 +372,19 @@
     dims,
     x_h, cot_h, q_h, k_h, v_h, c_h, nb_h, z1_h, r1_h, act_h, dg_h, z2_h, r2_h,
     wq_h, wk_h, wv_h, wo_h, wi_h, w2_h,
-    lse, seg_row, seg_col, dpool, g1, g2,
-    tok_o, douter_o, dinner_o, dout_o, dq_o, dk_o, dv_o, vec_o,
-    grads, *rest,
+    lse, seg, dpool, g1_in, g2_in,
+    grads, grad, vec_o,
+    *rest,
 ):
     S = len(dims)
     land, rest = rest[:S], rest[S:]
     (
-        b0, b1, b2, b3, b4, b5, b6, b7, b8, b9, b10, grad, rbuf, bias, vbuf, vrecv,
-        lsem, ssem, rsem, osem, vs, vr, freed, slot, tsem,
+        b0, b1, b2, b3, b4, b5, b6, b7, b8, b9, b10, rbuf, bias, gains, vbuf, vrecv,
+        lsem, ssem, rsem, vs, vr, freed, slot,
     ) = rest
     total, width = grads.shape
     rows = x_h.shape[0]
-    nrow = seg_row.shape[0]
+    nrow = seg.shape[0]
     seqlen = rows // nrow
     pairs = width // 128
     nff = w2_h.shape[0] // width
@@ -385,7 +392,7 @@
     CH = 8 << S
     C = total // CH
     NS = land[0].shape[0] // (CH // 2)
-    M = CH // UNIT
+    M = CH // 256
     route = Route(dims)
     bar = pltpu.get_barrier_semaphore()
 
@@ -444,6 +451,10 @@
     DQB, DVB, DOB, DNG, DNS, DIB = 0, 1, 2, 3, 4, 5
     D2B, DFG, DFS = DIB + nff, DIB + nff + 1, DIB + nff + 2
     vbuf[...] = jnp.zeros_like(vbuf)
+    g1 = gains.at[pl.ds(0, 1)]
+    g2 = gains.at[pl.ds(1, 1)]
+    g1[...] = g1_in[...].reshape(1, -1)
+    g2[...] = g2_in[...].reshape(1, -1)
 
     def vadd(i, value):
         vbuf[0, pl.ds(i, 1)] = vbuf[0, pl.ds(i, 1)] + value
@@ -451,7 +462,7 @@
     def second():
         kinds = lax.broadcasted_iota(jnp.int32, (S_ROW, seqlen), 0)
         for r in range(nrow):
-            onehot = (seg_row[r] == kinds).astype(F32)
+            onehot = (seg[r : r + 1] == kinds).astype(F32)
             count = jnp.sum(onehot, axis=1, keepdims=True)
             share = dpool[r * S_ROW : (r + 1) * S_ROW] / count
             grad[pl.ds(r * seqlen, seqlen)] = dot(onehot, share, 0, 0, HIGH)
@@ -574,7 +585,8 @@
     def attention(a):
         r = a // (pairs // 2)
         span = tile(r, seqlen)
-        bias[...] = jnp.where(seg_col[span] == seg_row[r], 0.0, masked_score).astype(F32)
+        line = seg[pl.ds(r, 1)]
+        bias[...] = jnp.where(column(line) == line, 0.0, masked_score).astype(F32)
 
         def pair(i, _):
             p = (a - r * (pairs // 2)) * 2 + i
@@ -653,111 +665,88 @@
         def _():
             token_part(t - T_TOK)
 
-        @pl.when(t == T_END)
-        def _():
-            pltpu.make_async_copy(grad, tok_o, tsem).start()
-
-    def offset(s, c):
+    def pieces(s):
+        if s == 0 or S != 5:
+            return [(0, width, 0)]
+        return [(0, width - NARROW, 0), (width - NARROW, NARROW, 1)]
+
+    def offset(s, c, colour):
         o = c * CH
         for k in range(s):
-            o = o + route.bit(k, colour_of(c)) * (CH >> (k + 1))
+            o = o + route.bit(k, colour) * (CH >> (k + 1))
         return o
 
-    def reduce_copy(s, c):
+    def reduce_copies(s, c):
         half = CH >> (s + 1)
-        b = route.bit(s, colour_of(c))
-        o = offset(s, c)
-        keep = pl.multiple_of(o + b * half, 8)
-        send = pl.multiple_of(o + (1 - b) * half, 8)
-        here = pl.multiple_of((c % NS) * half, 8)
-        cp = pltpu.make_async_remote_copy(
-            grads.at[pl.ds(send, half)], land[s].at[pl.ds(here, half)],
-            ssem.at[s, c], rsem.at[s, c],
-            device_id=route.partner(s, colour_of(c)), device_id_type=MESH,
-        )
-        return cp, keep, here, half
-
-    def gather_copy(s, c):
+        here = pl.ds(pl.multiple_of((c % NS) * half, 8), half)
+        for i, (x, w, colour) in enumerate(pieces(s)):
+            b = route.bit(s, colour)
+            o = offset(s, c, colour)
+            keep = pl.ds(pl.multiple_of(o + b * half, 8), half)
+            send = pl.ds(pl.multiple_of(o + (1 - b) * half, 8), half)
+            cols = pl.ds(x, w)
+            who = route.partner(s, colour)
+            cp = pltpu.make_async_remote_copy(
+                grads.at[send, cols], land[s].at[here, cols], ssem.at[s, c, i], rsem.at[s, c, i],
+                device_id=who, device_id_type=MESH,
+            )
+            yield cp, keep, here, cols, who, i
+
+    def gather_copies(s, c):
         half = CH >> (s + 1)
-        keep = pl.multiple_of(offset(s, c) + route.bit(s, colour_of(c)) * half, 8)
         rank = 2 * S - 1 - s
-        return pltpu.make_async_remote_copy(
-            grads.at[pl.ds(keep, half)], grads.at[pl.ds(keep, half)],
-            ssem.at[rank, c], rsem.at[rank, c],
-            device_id=route.partner(s, colour_of(c)), device_id_type=MESH,
-        )
-
-    per = width // UNIT
-
-    def out_copies(c, start):
-        for i in range(M):
-            unit = c * M + i
-            src = grads.at[pl.ds(pl.multiple_of(unit * UNIT, UNIT), UNIT)]
-            if not start:
-                pltpu.make_async_copy(src, dq_o.at[pl.ds(0, UNIT)], osem.at[unit]).wait()
-                continue
-            block = unit // per
-            line = pl.multiple_of((unit - block * per) * UNIT, UNIT)
-            for b in range(2 * nff + 4):
-                if b >= 2 * nff:
-                    dst = (dout_o, dq_o, dk_o, dv_o)[b - 2 * nff].at[pl.ds(line, UNIT)]
-                elif b % 2 == 0:
-                    dst = douter_o.at[pl.ds(b // 2 * width + line, UNIT)]
-                else:
-                    dst = dinner_o.at[pl.ds(line, UNIT), pl.ds(b // 2 * width, width)]
-
-                @pl.when(block == b)
-                def _():
-                    pltpu.make_async_copy(src, dst, osem.at[unit]).start()
+        for i, (x, w, colour) in enumerate(pieces(s)):
+            o = offset(s, c, colour) + route.bit(s, colour) * half
+            here = grads.at[pl.ds(pl.multiple_of(o, 8), half), pl.ds(x, w)]
+            yield pltpu.make_async_remote_copy(
+                here, here, ssem.at[rank, c, i], rsem.at[rank, c, i],
+                device_id=route.partner(s, colour), device_id_type=MESH,
+            ), i
 
     def start(p, c):
         if p < S:
-            @pl.when(c >= NS)
-            def _():
-                pl.semaphore_wait(slot.at[p, c], 1)
-
-            reduce_copy(p, c)[0].start()
-        elif p < 2 * S:
+            for cp, _, _, _, _, i in reduce_copies(p, c):
+                @pl.when(c >= NS)
+                def _():
+                    pl.semaphore_wait(slot.at[p, c, i], 1)
+
+                cp.start()
+        else:
             s = 2 * S - 1 - p
-            pl.semaphore_wait(freed.at[s, c], 1)
-            gather_copy(s, c).start()
-        else:
-            out_copies(c, True)
+            for cp, i in gather_copies(s, c):
+                pl.semaphore_wait(freed.at[s, c, i], 1)
+                cp.start()
 
     def finish(p, c):
         if p < S:
-            cp, keep, here, half = reduce_copy(p, c)
-            cp.wait_recv()
-            grads[pl.ds(keep, half)] = grads[pl.ds(keep, half)] + land[p][pl.ds(here, half)]
-            cp.wait_send()
-            pl.semaphore_signal(
-                freed.at[p, c], inc=1, device_id=route.partner(p, colour_of(c)), device_id_type=MESH
-            )
-
-            @pl.when(c + NS < C)
-            def _():
-                pl.semaphore_signal(
-                    slot.at[p, c + NS], inc=1,
-                    device_id=route.partner(p, colour_of(c + NS)), device_id_type=MESH,
-                )
-        elif p < 2 * S:
-            gather_copy(2 * S - 1 - p, c).wait()
+            for cp, keep, here, cols, who, i in reduce_copies(p, c):
+                cp.wait_recv()
+                grads[keep, cols] = grads[keep, cols] + land[p][here, cols]
+                cp.wait_send()
+                pl.semaphore_signal(freed.at[p, c, i], inc=1, device_id=who, device_id_type=MESH)
+
+                @pl.when(c + NS < C)
+                def _():
+                    pl.semaphore_signal(
+                        slot.at[p, c + NS, i], inc=1, device_id=who, device_id_type=MESH
+                    )
         else:
-            out_copies(c, False)
+            for cp, _ in gather_copies(2 * S - 1 - p, c):
+                cp.wait()
 
     def vec_copy(r):
         return pltpu.make_async_remote_copy(
             vbuf.at[r], vrecv.at[r], vs.at[r], vr.at[r], device_id=plain(r), device_id_type=MESH
         )
 
-    NP = 2 * S + 1
+    NP = 2 * S
 
     def at(t, p):
         if M == 1:
-            c = t - 2 * p
+            c = t - LAG * p
             return c, (c >= 0) & (c < C)
-        c = (t - 2 * p + 1) // M - 1
-        return c, (c >= 0) & (c < C) & ((c + 1) * M == t - 2 * p + 1)
+        c = (t - LAG * p + 1) // M - 1
+        return c, (c >= 0) & (c < C) & ((c + 1) * M == t - LAG * p + 1)
 
     def step(t, _):
         for p in range(NP):
@@ -769,7 +758,7 @@
                 vec_copy(r).start()
         slices(t)
         for p in range(NP):
-            c, valid = at(t - 1, p)
+            c, valid = at(t - FIN, p)
             pl.when(valid)(functools.partial(finish, p, c))
         for r in range(S):
             @pl.when(t == T_TOK + 1 + 2 * r)
@@ -782,9 +771,8 @@
     second()
     ffn_outer(0)
     pl.semaphore_wait(bar, S)
-    steps = max(C * M + 2 * (NP - 1) + 1, T_TOK + 2 * S, T_END + 1)
+    steps = max(C * M + LAG * (NP - 1) + FIN, T_TOK + 2 * S, T_END + 1)
     lax.fori_loop(0, steps, step, 0)
-    pltpu.make_async_copy(grad, tok_o, tsem).wait()
     vec_o[...] = vbuf[S]
 
 
@@ -801,41 +789,82 @@
     CH = 8 << S
     total = (2 * nff + 4) * width
     C = total // CH
-    NS = max(2, 2048 // CH)
+    NS = max(1, 1024 // CH)
     nvec = -(-(8 + nff) // 8) * 8
     vm = pl.BlockSpec(memory_space=pltpu.VMEM)
     hbm = pl.BlockSpec(memory_space=pl.ANY)
     sd = jax.ShapeDtypeStruct
     dma = pltpu.SemaphoreType.DMA
     plain = pltpu.SemaphoreType.REGULAR
-    full = sd((width, width), F32)
-    row = lambda a: a.reshape(1, -1)
     return pl.pallas_call(
         functools.partial(backward_kernel, dims),
         name="backward_reduce",
         out_shape=(
-            sd((rows, width), F32), sd((inner, width), F32), sd((width, inner), F32),
-            full, full, full, full, sd((nvec, width), F32),
+            pltpu.VMEM((total, width), F32), sd((rows, width), F32), sd((nvec, width), F32),
         ),
-        in_specs=[hbm] * 19 + [vm] * 6,
-        out_specs=[hbm] * 7 + [vm],
-        scratch_shapes=[pltpu.VMEM((total, width), F32)]
-        + [pltpu.VMEM((NS * (CH >> (s + 1)), width), F32) for s in range(S)]
+        in_specs=[hbm] * 19 + [vm] * 5,
+        out_specs=[vm, vm, vm],
+        scratch_shapes=[pltpu.VMEM((NS * (CH >> (s + 1)), width), F32) for s in range(S)]
         + [pltpu.VMEM((rows, width), BF)] * 11
         + [
-            pltpu.VMEM((rows, width), F32), pltpu.VMEM((rows, 128), F32),
-            pltpu.VMEM((seqlen, seqlen), F32), pltpu.VMEM((S + 1, nvec, width), F32),
+            pltpu.VMEM((rows, 128), F32), pltpu.VMEM((seqlen, seqlen), F32),
+            pltpu.VMEM((8, width), F32), pltpu.VMEM((S + 1, nvec, width), F32),
             pltpu.VMEM((S, nvec, width), F32),
-            dma((4 * nff + 15,)), dma((2 * S, C)), dma((2 * S, C)), dma((total // UNIT,)),
-            dma((S,)), dma((S,)), plain((S, C)), plain((S, C)), dma,
+            dma((4 * nff + 15,)), dma((2 * S, C, 2)), dma((2 * S, C, 2)),
+            dma((S,)), dma((S,)), plain((S, C, 2)), plain((S, C, 2)),
         ],
         compiler_params=pltpu.CompilerParams(
-            collective_id=1, has_side_effects=True, vmem_limit_bytes=67043328
+            collective_id=1, has_side_effects=True, vmem_limit_bytes=VMEM_KERNEL
         ),
     )(
-        tokens, cotangent, *kept, wq, wk, wv, wo, wi, w2, lse,
-        segment.reshape(nrow, 1, seqlen), segment.reshape(rows, 1), dpooled, row(g1), row(g2),
+        tokens, cotangent, *kept, wq, wk, wv, wo, wi, w2, lse, segment, dpooled, g1, g2,
     )
+
+
+def write_kernel(nff, grads, grad, vec, douter, dinner, dout, dq, dk, dv, tok, *rest):
+    sem = rest[-1]
+    rest = rest[:-1]
+    width = grads.shape[1]
+
+    def block(b):
+        return grads.at[pl.ds(b * width, width)]
+
+    copies = [(grad, tok)]
+    for j in range(nff):
+        copies.append((block(2 * j), douter.at[pl.ds(j * width, width)]))
+        copies.append((block(2 * j + 1), dinner.at[:, pl.ds(j * width, width)]))
+    for i, dst in enumerate((dout, dq, dk, dv)):
+        copies.append((block(2 * nff + i), dst))
+    copies = [pltpu.make_async_copy(a, b, sem.at[i]) for i, (a, b) in enumerate(copies)]
+    for c in copies:
+        c.start()
+    at = 0
+    for dst in rest:
+        for j in range(dst.shape[0] // width):
+            dst[pl.ds(j * width, width)] = vec[at]
+            at += 1
+    for c in copies:
+        c.wait()
+
+
+def write_out(grads, grad, vec, inner):
+    width = grads.shape[1]
+    nff = inner // width
+    sd = jax.ShapeDtypeStruct
+    hbm = pl.BlockSpec(memory_space=pl.ANY)
+    vm = pl.BlockSpec(memory_space=pltpu.VMEM)
+    full = sd((width, width), F32)
+    line = sd((width,), F32)
+    return pl.pallas_call(
+        functools.partial(write_kernel, nff),
+        name="write_out",
+        out_shape=[sd((inner, width), F32), sd((width, inner), F32), full, full, full, full]
+        + [sd(grad.shape, F32)] + [line] * 5 + [sd((inner,), F32)] + [line] * 3,
+        in_specs=[hbm, hbm, vm],
+        out_specs=[hbm] * 7 + [vm] * 9,
+        scratch_shapes=[pltpu.SemaphoreType.DMA((2 * nff + 5,))],
+        compiler_params=pltpu.CompilerParams(vmem_limit_bytes=4000000),
+    )(grads, grad, vec)
 
 
 def local(
@@ -844,7 +873,6 @@
     value_bias, out_weight, out_bias, norm_gain, norm_shift, inner_weight, inner_bias,
     outer_weight, outer_bias, final_gain, final_shift,
 ):
-    width = tokens.shape[1]
     (
         query_b, key_b, value_b, context_b, normed_b, z1, r1, active_b, slope, z2, r2, lse,
         layer_out, pooled,
@@ -859,20 +887,15 @@
         query_b, key_b, value_b, context_b, normed_b, z1, r1, active_b, slope, z2, r2,
     )
     weights = (query_weight, key_weight, value_weight, out_weight, inner_weight, outer_weight)
-    (
-        tokens_grad, douter_weight, dinner_weight, dout_weight, dquery_weight, dkey_weight,
-        dvalue_weight, packed,
-    ) = backward_reduce(
+    grads, grad, packed = backward_reduce(
         tokens, cotangent, kept, weights, lse, segment, dpooled, norm_gain, final_gain,
         dp_size, bucket_size,
     )
-    packed = packed.reshape(-1)
-    sizes = [width] * 5 + [inner_bias.shape[0]] + [width] * 3
-    ends = [sum(sizes[: i + 1]) for i in range(len(sizes))]
     (
-        dquery_bias, dvalue_bias, dout_bias, dnorm_gain, dnorm_shift,
-        dinner_bias, douter_bias, dfinal_gain, dfinal_shift,
-    ) = (packed[e - n : e] for e, n in zip(ends, sizes))
+        douter_weight, dinner_weight, dout_weight, dquery_weight, dkey_weight, dvalue_weight,
+        tokens_grad, dquery_bias, dvalue_bias, dout_bias, dnorm_gain, dnorm_shift, dinner_bias,
+        douter_bias, dfinal_gain, dfinal_shift,
+    ) = write_out(grads, grad, packed, inner_bias.shape[0])
     return (
         layer_out, loss_value, tokens_grad, dquery_weight, dquery_bias, dkey_weight,
         dvalue_weight, dvalue_bias, dout_weight, dout_bias, dnorm_gain, dnorm_shift,

time: 387 us -> 352 us (0.910)
  local copies, waits for them, and re-layouts: 40.6 us -> 2.68 us
    unnamed x29 -> x4, local copies, waits for them, and re-layouts: 24.5 us -> 2.68 us
    reshape x10 -> x0, local copies, waits for them, and re-layouts: 12.9 us -> none  [the longest x8 10.1 us: forward(): row = lambda a: a.reshape(1, -1)]
    pallas_call x0 -> x1, Pallas kernels: none -> 11 us  [write_out(): pl.pallas_call(functools.partial(write_kernel, nff), name='write_out', ou...]
    pallas_call x1, Pallas kernels: 260 us -> 251 us  [backward_reduce(): pl.pallas_call(functools.partial(backward_kernel, dims), name='backward_r...]
where the time goes in v4:
time: 352 us; the launch traced here: 351 us
  Pallas kernels  346 us (98%)
    pallas_call x1, Pallas kernels, backward_reduce(): pl.pallas_call(functools.partial(backward_kernel, dims), name='backward_r...  251 us
    pallas_call x1, Pallas kernels, forward(): pl.pallas_call(forward_kernel, name='forward', out_shape=outs, in_specs=[...  50.2 us
    pallas_call x1, Pallas kernels, pair_loss(): pl.pallas_call(functools.partial(loss_kernel, dims, bucket_size), name='p...  34.4 us
    pallas_call x1, Pallas kernels, write_out(): pl.pallas_call(functools.partial(write_kernel, nff), name='write_out', ou...  11 us

profile of v4, /device:TPU:0, one launch (start us, length us, event | category | flops | bytes accessed | tf_op | source)
XLA Modules:
  0.0 351.5 jit_solution(7926121755500290696)
XLA Ops:
  0.7 50.2 %forward.1 = (bf16[1024,768]{1,0:T(8,128)(2,1)}, bf16[1024,768]{1,0:T(8,128)(2,1)}, bf16[1024,768]{1,0:T(8,128)(2,1)}, bf16[1024,768]{1,0:T(8,128)(2,1)}, bf16[1...) custom-call(bf16[1024,768]{1,0:T(8,128)(2,1)} %x_h.1, ...), custom_call_target="tpu_custom_call" | custom-call | tf_op jit(solution)/shard_map/forward/pallas_call | solution.py:196
  50.8 34.4 %pair_loss.1 = (f32[16,768]{1,0:T(8,128)}, f32[1,1]{1,0:T(1,128)}) custom-call(f32[16,768]{1,0:T(8,128)} %get-tuple-element.54.pool, s32[1,512]{1,0:T(1,128)} %constant.2.clone.sid, s32[512]{0:T(512)} %order.1), custom_call_target="tpu_custom_call" | custom-call | tf_op jit(solution)/shard_map/pair_loss/pallas_call | solution.py:343
  85.2 250.8 %backward_reduce.1 = (f32[9216,768]{1,0:T(8,128)S(1)}, f32[1024,768]{1,0:T(8,128)}, f32[16,768]{1,0:T(8,128)}) custom-call(bf16[1024,768]{1,0:T(8,128)(2,1)} %x_h.1, bf16[1024,768]{1,0:T(8,128)(2,1)} %cot_h.1, bf16[1024,768]{1,0:T(8,128)(2,1)} %get-tuple-element.56.q_h, bf16[1024,768]{1,0:T(8,128)(2,1)} %get-tuple-element.57.k_h, ...), custom_call_target="tpu_custom_call" | custom-call | tf_op jit(solution)/shard_map/backward_reduce/pallas_call | solution.py:799
  336.1 0.0 copy-start
  336.1 1.9 copy-done
  337.9 0.0 copy-start.1
  337.9 0.8 copy-done.1
  338.7 11.0 %write_out.1 = (f32[3072,768]{1,0:T(8,128)}, f32[768,3072]{1,0:T(8,128)}, f32[768,768]{1,0:T(8,128)}, f32[768,768]{1,0:T(8,128)}, f32[768,768]{1,0:T(8,128)}, /*...) custom-call(f32[9216,768]{1,0:T(8,128)S(1)} %get-tuple-element.69.gr, ...), custom_call_target="tpu_custom_call" | custom-call | tf_op jit(solution)/shard_map/write_out/pallas_call | solution.py:858
Async XLA Ops:
  336.1 1.9 copy-start
  337.9 0.8 copy-start.1
